TPU v7x, 256 devices: a whole 4x4x8 slice. The times are simulated.
256 devices in a mesh: ctx: 16 (over y_hi, z), tp: 8 (over x, y_lo), probe: 2 (over core).
Axes of the slice: x: 4, y: 4 (y_hi: 2, y_lo: 2; y = y_hi * 2 + y_lo), z: 8, core: 2. Of those that a mesh axis runs over, the one named last changes fastest.
Arguments:
- latent: float32 [2048, 3072], P('ctx', 'tp'), may hold values from -6 to 6
- probes: int32 [2, 2048, 3072], P('probe', 'ctx', 'tp'), may hold values from 0 to 1
- modulation: float32 [2, 3, 3072], replicated, may hold values from -3 to 3
- pattern: int32 [16, 8], P('ctx'), may hold values from 0 to 15, as said below
- w_qkv: bfloat16 [3072, 3, 3072], P(None, None, 'tp'), may hold values from -0.109375 to 0.109375
- w_out: bfloat16 [3072, 3072], P('tp'), may hold values from -0.109375 to 0.109375
- w_up: bfloat16 [3072, 6144], P('ctx', 'tp'), may hold values from -0.109375 to 0.109375
- w_down: bfloat16 [6144, 3072], P('tp', 'ctx'), may hold values from -0.078125 to 0.078125
- q_gain: float32 [3072], P('tp'), may hold values from 0.5 to 5.1, as said below
- k_gain: float32 [3072], P('tp'), may hold values from 0.5 to 2
Outputs:
- latent_out: float32 [2048, 3072], P('ctx', 'tp')
- density_change: float32 [2048], P('ctx')
Inputs may be any that keep to these rules, and one draw needn't show every extreme that they name: `pattern`: row q lists key blocks for query block q: its first entry is q; the next entries are distinct blocks other than q up to a count of 1 to 8, after which every entry is q again; row 0 lists 8 distinct blocks. `q_gain`: positive gains.
All inputs are finite; a program needn't handle non-finite values.
Results may differ from a plain program's by a relative error of at most 0.034.
Values may be sent and summed in bfloat16 or wider, within the bound.
A program may use at most 128 MiB of HBM per device.

v0:
```python
from functools import partial
import math

import jax
import jax.numpy as jnp
from jax import lax
from jax.sharding import PartitionSpec as P

HD = 128
BLK = 128
K_SEL = 8
STEPS = 2


EPS = 1e-06
NEG_BIG = -1e30


def norm_features(rows, tangent, shift, stretch, full_width):
    row_sums = jnp.stack(
        [jnp.sum(rows, 1), jnp.sum(rows * rows, 1), jnp.sum(tangent, 1), jnp.sum(rows * tangent, 1)]
    )
    totals = lax.psum(row_sums, "tp")
    row_mean = totals[0][:, None] / full_width
    row_var = totals[1][:, None] / full_width - row_mean * row_mean
    tan_mean = totals[2][:, None] / full_width
    tan_var = 2.0 * (totals[3][:, None] / full_width - row_mean * tan_mean)
    inv_std = lax.rsqrt(row_var + EPS)
    centred = rows - row_mean
    normed = centred * inv_std
    tan_normed = (
        tangent - tan_mean
    ) * inv_std - 0.5 * centred * inv_std * inv_std * inv_std * tan_var
    normed_act = (normed * (1.0 + stretch) + shift).astype(jnp.bfloat16)
    tangent_act = (tan_normed * (1.0 + stretch)).astype(jnp.bfloat16)
    return (
        lax.all_gather(normed_act, "tp", axis=1, tiled=True),
        lax.all_gather(tangent_act, "tp", axis=1, tiled=True),
    )


def head_rms(projected, tan_projected, head_gain):
    row_count = projected.shape[0]
    heads_local = head_gain.shape[0] // HD
    head_view = projected.reshape(row_count, heads_local, HD)
    tan_view = tan_projected.reshape(row_count, heads_local, HD)
    gain_view = head_gain.reshape(heads_local, HD)
    inv_std = lax.rsqrt(jnp.mean(head_view * head_view, axis=-1, keepdims=True) + EPS)
    tan_inv = -inv_std * inv_std * inv_std * jnp.mean(head_view * tan_view, axis=-1, keepdims=True)
    result = (head_view * inv_std * gain_view).astype(jnp.bfloat16)
    tan_result = ((tan_view * inv_std + head_view * tan_inv) * gain_view).astype(jnp.bfloat16)
    return (result, tan_result)


def empty_carry(heads_local, row_count):
    return (
        jnp.full((heads_local, row_count), NEG_BIG, jnp.float32),
        jnp.zeros((heads_local, row_count), jnp.float32),
        jnp.zeros((heads_local, row_count, HD), jnp.float32),
        jnp.zeros((heads_local, row_count, HD), jnp.float32),
        jnp.zeros((heads_local, row_count), jnp.float32),
    )


def attend(state_carry, query, key_set, allowed):
    running_max, run_total, run_acc, tan_acc, tan_sum = state_carry
    q_rows, dq_rows = query
    k_rows, v_rows, dk_rows, dv_rows = key_set
    score_scale = 1.0 / math.sqrt(q_rows.shape[2])
    scores = (
        jnp.einsum("qhd,khd->hqk", q_rows, k_rows, preferred_element_type=jnp.float32) * score_scale
    )
    tan_scores = (
        jnp.einsum("qhd,khd->hqk", dq_rows, k_rows, preferred_element_type=jnp.float32)
        + jnp.einsum("qhd,khd->hqk", q_rows, dk_rows, preferred_element_type=jnp.float32)
    ) * score_scale
    key_mask = allowed[None, :, :]
    scores = jnp.where(key_mask, scores, NEG_BIG)
    new_max = jnp.maximum(running_max, jnp.max(scores, axis=2))
    weights = jnp.where(key_mask, jnp.exp(scores - new_max[:, :, None]), 0.0)
    values = v_rows.astype(jnp.float32)
    tan_values = dv_rows.astype(jnp.float32)
    weighted_ds = weights * tan_scores
    run_total = jnp.sum(weights, axis=2)
    run_acc = jnp.einsum("hqk,khd->hqd", weights, values, precision=lax.Precision.HIGHEST)
    tan_acc = jnp.einsum(
        "hqk,khd->hqd", weights, tan_values, precision=lax.Precision.HIGHEST
    ) + jnp.einsum("hqk,khd->hqd", weighted_ds, values, precision=lax.Precision.HIGHEST)
    tan_sum = jnp.sum(weighted_ds, axis=2)
    return (new_max, run_total, run_acc, tan_acc, tan_sum)


def finish(state_carry):
    running_max, run_total, run_acc, tan_acc, tan_sum = state_carry
    output = run_acc / run_total[:, :, None]
    tan_output = tan_acc / run_total[:, :, None] - (tan_sum / run_total)[:, :, None] * output
    heads_local, row_count, head_size = output.shape
    output = (
        output.transpose(1, 0, 2).reshape(row_count, heads_local * head_size).astype(jnp.bfloat16)
    )
    tan_output = (
        tan_output.transpose(1, 0, 2)
        .reshape(row_count, heads_local * head_size)
        .astype(jnp.bfloat16)
    )
    return (output, tan_output)


def select_blocks(whole_rows, chosen, block_total, heads_local):
    blocked = whole_rows.reshape(block_total, BLK, heads_local * HD)
    return jnp.take(blocked, chosen, axis=0).reshape(K_SEL * BLK, heads_local, HD)


def listed_attention(q_rows, dq_rows, whole_set, pattern, block_total, heads_local):
    chosen = pattern[0]
    valid_cols = (jnp.arange(K_SEL) == 0) | (chosen != chosen[0])
    allowed = jnp.broadcast_to(jnp.repeat(valid_cols, BLK)[None, :], (BLK, K_SEL * BLK))
    key_set = tuple(
        (select_blocks(member, chosen, block_total, heads_local) for member in whole_set)
    )
    query = (q_rows[0:BLK], dq_rows[0:BLK])
    block_out, block_tan = finish(attend(empty_carry(heads_local, BLK), query, key_set, allowed))
    return (block_out, block_tan)


def local(latent, probes, modulation, pattern, w_qkv, w_out, w_up, w_down, q_gain, k_gain):
    row_count, local_width = latent.shape
    full_width = local_width * lax.axis_size("tp")
    feature_start = lax.axis_index("tp") * local_width
    heads_local = q_gain.shape[0] // HD
    block_total = row_count * lax.axis_size("ctx") // BLK
    step_size = 1.0 / STEPS
    probe_signs = 2.0 * probes[0].astype(jnp.float32) - 1.0
    up_full, down_full = (
        lax.all_gather(w_up, "ctx", axis=0, tiled=True),
        lax.all_gather(w_down, "ctx", axis=1, tiled=True),
    )
    gelu_tanh = partial(jax.nn.gelu, approximate=True)
    change = jnp.zeros((row_count,), jnp.float32)
    for euler_step in range(STEPS):
        mod_local = lax.dynamic_slice_in_dim(modulation[euler_step], feature_start, local_width, 1)
        normed_act, tangent_act = norm_features(
            latent, probe_signs, mod_local[0], mod_local[1], full_width
        )
        stacked = jnp.concatenate([normed_act, tangent_act], axis=0)
        projected = jnp.einsum("rd,dcf->crf", stacked, w_qkv, preferred_element_type=jnp.float32)
        q_rows, dq_rows = head_rms(projected[0, :row_count], projected[0, row_count:], q_gain)
        k_heads, dk_heads = head_rms(projected[1, :row_count], projected[1, row_count:], k_gain)
        k_rows = k_heads.reshape(row_count, heads_local * HD)
        dk_rows = dk_heads.reshape(row_count, heads_local * HD)
        v_rows = projected[2, :row_count].astype(jnp.bfloat16)
        dv_rows = projected[2, row_count:].astype(jnp.bfloat16)
        k_whole, v_whole, dk_whole, dv_whole = (
            lax.all_gather(k_rows, "ctx", axis=0, tiled=True),
            lax.all_gather(v_rows, "ctx", axis=0, tiled=True),
            lax.all_gather(dk_rows, "ctx", axis=0, tiled=True),
            lax.all_gather(dv_rows, "ctx", axis=0, tiled=True),
        )
        attended, tan_attended = listed_attention(
            q_rows,
            dq_rows,
            (k_whole, v_whole, dk_whole, dv_whole),
            pattern,
            block_total,
            heads_local,
        )
        pre_hidden = jnp.dot(stacked, up_full, preferred_element_type=jnp.float32)
        hidden, tan_hidden = jax.jvp(
            gelu_tanh, (pre_hidden[:row_count],), (pre_hidden[row_count:],)
        )
        attn_rows = jnp.concatenate([attended, tan_attended], axis=0)
        mlp_rows = jnp.concatenate(
            [hidden.astype(jnp.bfloat16), tan_hidden.astype(jnp.bfloat16)], axis=0
        )
        partials = jnp.dot(attn_rows, w_out, preferred_element_type=jnp.float32) + jnp.dot(
            mlp_rows, down_full, preferred_element_type=jnp.float32
        )
        summed = lax.psum_scatter(
            partials.astype(jnp.bfloat16), "tp", scatter_dimension=1, tiled=True
        ).astype(jnp.float32)
        speed = mod_local[2] * summed[:row_count]
        tan_speed = mod_local[2] * summed[row_count:]
        change = change + jnp.sum(probe_signs * tan_speed, axis=1)
        latent = latent + step_size * speed
    total_change = lax.psum(change, ("tp", "probe"))
    density_change = -step_size * total_change / (lax.axis_size("probe") * math.sqrt(full_width))
    return (latent, density_change)


def solution(mesh):
    return jax.shard_map(
        local,
        mesh=mesh,
        in_specs=(
            P("ctx", "tp"),
            P("probe", "ctx", "tp"),
            P(),
            P("ctx", None),
            P(None, None, "tp"),
            P("tp", None),
            P("ctx", "tp"),
            P("tp", "ctx"),
            P("tp"),
            P("tp"),
        ),
        out_specs=(P("ctx", "tp"), P("ctx")),
        check_vma=False,
    )
```

profile of v0, /device:TPU:1, one launch (start us, length us, event | category | flops | bytes accessed | tf_op | source)
XLA Modules:
  0.0 1214.0 jit_solution(16724503533342251219)
XLA Ops:
  9.6 16.8 %psum.21 = f32[4,128]{1,0:T(4,128)S(1)} all-reduce(f32[4,128]{1,0:T(4,128)S(1)} %fusion.105), channel_id=1, replica_groups=mesh['ctx'=16,'tp'=8,'probe'=2] {'tp'}, use_global_device_ids=true, to_apply=%region_4.0 | all-reduce | flops 512 | bytes 4096 | tf_op jit(solution)/shard_map/psum | solution.py:23
  29.3 25.0 %all_gather.43 = bf16[128,3072]{1,0:T(8,128)(2,1)S(1)} all-gather(bf16[128,384]{1,0:T(8,128)(2,1)S(1)} %get-tuple-element.49), channel_id=1, replica_groups=mesh['ctx'=16,'tp'=8,'probe'=2] {'tp'}, dimensions={1}, use_global_device_ids=true | all-gather | bytes 884736 | tf_op jit(solution)/shard_map/all_gather | solution.py:38
  54.4 24.5 %all_gather.42 = bf16[128,3072]{1,0:T(8,128)(2,1)S(1)} all-gather(bf16[128,384]{1,0:T(8,128)(2,1)S(1)} %get-tuple-element.50), channel_id=1, replica_groups=mesh['ctx'=16,'tp'=8,'probe'=2] {'tp'}, dimensions={1}, use_global_device_ids=true | all-gather | bytes 884736 | tf_op jit(solution)/shard_map/all_gather | solution.py:37
  79.0 5.8 fusion.135
  105.8 74.2 %all-gather.27.cloned.1.call-done = bf16[1,2048,384]{2,1,0:T(8,128)(2,1)} async-done(((bf16[1,128,384]{2,1,0:T(8,128)(2,1)}), bf16[1,2048,384]{2,1,0:T(8,128)(2,1)}) %all-gather.27.cloned.1.call-update) | async-done | bytes 1572880 | tf_op jit(solution)/shard_map/all_gather | solution.py:155
  180.0 2.1 gather_fusion.1
  182.1 79.4 %all-gather.29.cloned.1.call-done = bf16[1,2048,384]{2,1,0:T(8,128)(2,1)} async-done(((bf16[1,128,384]{2,1,0:T(8,128)(2,1)}), bf16[1,2048,384]{2,1,0:T(8,128)(2,1)}) %all-gather.29.cloned.1.call-update) | async-done | bytes 1572880 | tf_op jit(solution)/shard_map/all_gather | solution.py:157
  261.5 3.0 gather_fusion.2
  264.5 79.1 %all-gather.17.cloned.1.call-done = bf16[2048,384]{1,0:T(8,128)(2,1)} async-done(((bf16[128,384]{1,0:T(8,128)(2,1)}), bf16[2048,384]{1,0:T(8,128)(2,1)}) %all-gather.17.cloned.1.call-update) | async-done | bytes 1572880 | tf_op jit(solution)/shard_map/all_gather | solution.py:156
  343.6 2.9 gather_fusion.3
  346.5 78.4 %all-gather.15.cloned.1.call-done = bf16[2048,384]{1,0:T(8,128)(2,1)} async-done(((bf16[128,384]{1,0:T(8,128)(2,1)}), bf16[2048,384]{1,0:T(8,128)(2,1)}) %all-gather.15.cloned.1.call-update) | async-done | bytes 1572880 | tf_op jit(solution)/shard_map/all_gather | solution.py:154
  424.9 3.0 gather_fusion
  427.9 3.4 broadcast_select_fusion.6
  434.2 2.5 copy.97
  436.8 2.2 reshape.367
  441.7 3.2 reshape.476
  451.8 76.6 %all-gather.19.cloned.1.call-done = bf16[3072,768]{1,0:T(8,128)(2,1)} async-done(((bf16[192,768]{1,0:T(8,128)(2,1)}), bf16[3072,768]{1,0:T(8,128)(2,1)}) %all-gather.19.cloned.1.call-update) | async-done | bytes 4718608 | tf_op jit(solution)/shard_map/all_gather | solution.py:135
  528.4 4.2 fusion.143
  532.9 98.5 %all-gather.21.cloned.1.call-done = bf16[768,3072]{0,1:T(8,128)(2,1)} async-done(((bf16[768,192]{0,1:T(8,128)(2,1)}), bf16[768,3072]{0,1:T(8,128)(2,1)}) %all-gather.21.cloned.1.call-update) | async-done | bytes 4718608 | tf_op jit(solution)/shard_map/all_gather | solution.py:136
  631.3 3.7 fusion.54
  635.1 2.2 fusion
  637.2 2.6 copy.142
  641.3 42.1 %reduce-scatter.7.cloned.1.call-done = bf16[384,256]{1,0:T(8,128)(2,1)} async-done(((bf16[3072,256]{1,0:T(8,128)(2,1)}), bf16[384,256]{1,0:T(8,128)(2,1)}) %reduce-scatter.7.cloned.1.call-update) | async-done | bytes 196624
  684.7 14.6 %psum.22 = f32[4,128]{1,0:T(4,128)S(1)} all-reduce(f32[4,128]{1,0:T(4,128)S(1)} %fusion.106), channel_id=1, replica_groups=mesh['ctx'=16,'tp'=8,'probe'=2] {'tp'}, use_global_device_ids=true, to_apply=%region_16.18 | all-reduce | flops 512 | bytes 4096 | tf_op jit(solution)/shard_map/psum | solution.py:23
  699.6 24.3 %all_gather.51 = bf16[128,3072]{1,0:T(8,128)(2,1)S(1)} all-gather(bf16[128,384]{1,0:T(8,128)(2,1)S(1)} %get-tuple-element.47), channel_id=1, replica_groups=mesh['ctx'=16,'tp'=8,'probe'=2] {'tp'}, dimensions={1}, use_global_device_ids=true | all-gather | bytes 884736 | tf_op jit(solution)/shard_map/all_gather | solution.py:38
  723.8 24.5 %all_gather.50 = bf16[128,3072]{1,0:T(8,128)(2,1)S(1)} all-gather(bf16[128,384]{1,0:T(8,128)(2,1)S(1)} %get-tuple-element.48), channel_id=1, replica_groups=mesh['ctx'=16,'tp'=8,'probe'=2] {'tp'}, dimensions={1}, use_global_device_ids=true | all-gather | bytes 884736 | tf_op jit(solution)/shard_map/all_gather | solution.py:37
  748.4 6.8 fusion.139
  756.8 2.0 slice_multiply_fusion.4
  763.9 4.3 fusion.144
  768.6 3.1 fusion.58
  771.6 79.8 %all-gather.31.cloned.1.call-done = bf16[1,2048,384]{2,1,0:T(8,128)(2,1)} async-done(((bf16[1,128,384]{2,1,0:T(8,128)(2,1)}), bf16[1,2048,384]{2,1,0:T(8,128)(2,1)}) %all-gather.31.cloned.1.call-update) | async-done | bytes 1572880 | tf_op jit(solution)/shard_map/all_gather | solution.py:155
  851.4 2.2 gather_fusion.5
  853.6 79.3 %all-gather.33.cloned.1.call-done = bf16[1,2048,384]{2,1,0:T(8,128)(2,1)} async-done(((bf16[1,128,384]{2,1,0:T(8,128)(2,1)}), bf16[1,2048,384]{2,1,0:T(8,128)(2,1)}) %all-gather.33.cloned.1.call-update) | async-done | bytes 1572880 | tf_op jit(solution)/shard_map/all_gather | solution.py:157
  932.9 3.1 gather_fusion.6
  936.0 78.3 %all-gather.25.cloned.1.call-done = bf16[2048,384]{1,0:T(8,128)(2,1)} async-done(((bf16[128,384]{1,0:T(8,128)(2,1)}), bf16[2048,384]{1,0:T(8,128)(2,1)}) %all-gather.25.cloned.1.call-update) | async-done | bytes 1572880 | tf_op jit(solution)/shard_map/all_gather | solution.py:156
  1014.2 3.1 gather_fusion.7
  1017.3 78.4 %all-gather.23.cloned.1.call-done = bf16[2048,384]{1,0:T(8,128)(2,1)} async-done(((bf16[128,384]{1,0:T(8,128)(2,1)}), bf16[2048,384]{1,0:T(8,128)(2,1)}) %all-gather.23.cloned.1.call-update) | async-done | bytes 1572880 | tf_op jit(solution)/shard_map/all_gather | solution.py:154
  1095.8 3.1 gather_fusion.4
  1098.8 3.5 broadcast_select_fusion.2
  1102.3 2.5 copy.113
  1104.9 2.2 reshape.373
  1109.8 2.4 copy.114
  1112.2 2.2 reshape.375
  1114.4 3.2 reshape.477
  1124.2 2.2 fusion.1
  1126.4 2.6 copy.144
  1129.1 44.3 %reduce-scatter.9.cloned.1.call-done = bf16[384,256]{1,0:T(8,128)(2,1)} async-done(((bf16[3072,256]{1,0:T(8,128)(2,1)}), bf16[384,256]{1,0:T(8,128)(2,1)}) %reduce-scatter.9.cloned.1.call-update) | async-done | bytes 196624
  1176.2 30.4 %psum.23 = f32[128]{0:T(128)S(1)} all-reduce(f32[128]{0:T(128)S(1)} %add.227), channel_id=1, replica_groups=mesh['ctx'=16,'tp'=8,'probe'=2] {'tp','probe'}, use_global_device_ids=true, to_apply=%region_27.29 | all-reduce | flops 128 | bytes 1024 | tf_op jit(solution)/shard_map/psum | solution.py:185
  (173 shorter events, 61.4 us)
Async XLA Ops:
  7.2 627.9 %copy-start = (bf16[384,3072]{1,0:T(8,128)(2,1)S(1)}, bf16[384,3072]{1,0:T(8,128)(2,1)}, u32[]{:S(2)}) copy-start(bf16[384,3072]{1,0:T(8,128)(2,1)} %param.17) | copy-start | bytes 7077892
  7.2 172.8 %all-gather.27.cloned.1.call-start = ((), (), s32[]{:S(2)}) async-start(), calls=%async_computation.8 | async-start | bytes 1671168 | tf_op jit(solution)/shard_map/all_gather | solution.py:155
  8.4 1.2 copy-start.26
  79.0 5.8 copy-start.17
  85.6 175.9 %all-gather.29.cloned.1.call-start = ((), (), s32[]{:S(2)}) async-start(), calls=%async_computation.9 | async-start | bytes 1671168 | tf_op jit(solution)/shard_map/all_gather | solution.py:157
  86.3 257.3 %all-gather.17.cloned.1.call-start = ((), (), s32[]{:S(2)}) async-start(), calls=%async_computation.3 | async-start | bytes 1671168 | tf_op jit(solution)/shard_map/all_gather | solution.py:156
  87.3 11.5 copy-start.21
  96.3 8.1 copy-start.28
  100.5 324.4 %all-gather.15.cloned.1.call-start = ((), (), s32[]{:S(2)}) async-start(), calls=%async_computation.2 | async-start | bytes 1671168 | tf_op jit(solution)/shard_map/all_gather | solution.py:154
  101.1 427.2 %all-gather.19.cloned.1.call-start = ((), (), s32[]{:S(2)}) async-start(), calls=%async_computation.4 | async-start | bytes 5013504 | tf_op jit(solution)/shard_map/all_gather | solution.py:135
  101.7 529.6 %all-gather.21.cloned.1.call-start = ((), (), s32[]{:S(2)}) async-start(), calls=%async_computation.5 | async-start | bytes 5013504 | tf_op jit(solution)/shard_map/all_gather | solution.py:136
  102.3 581.1 %reduce-scatter.7.cloned.1.call-start = ((), (), s32[]{:S(2)}) async-start(), calls=%async_computation.12 | async-start | bytes 1769472
  104.5 320.5 %copy-start.20 = (s32[1024]{0:T(1024)}, s32[1024]{0:T(1024)S(1)}, u32[]{:S(2)}) copy-start(s32[1024]{0:T(1024)S(1)} %pad_clamp_fusion) | copy-start | bytes 12292
  434.2 4.7 copy-start.5
  440.3 4.7 copy-start.19
  445.0 1.0 copy-start.25
  446.0 1.2 copy-start.4
  447.2 1.1 copy-start.15
  448.1 1.5 copy-start.8
  639.8 44.7 %copy-start.2 = (s32[1,128,384]{2,1,0:T(8,128)S(1)}, s32[1,128,384]{2,1,0:T(8,128)}, u32[]{:S(2)}) copy-start(s32[1,128,384]{2,1,0:T(8,128)} %param.13) | copy-start | bytes 589828
  639.8 44.7 %copy-start.11 = (f32[128,384]{1,0:T(8,128)S(1)}, f32[128,384]{1,0:T(8,128)}, u32[]{:S(2)}) copy-start(f32[128,384]{1,0:T(8,128)} %param.12) | copy-start | bytes 589828
  639.8 44.9 %copy-start.27 = (f32[128]{0:T(128)S(1)}, f32[128]{0:T(128)}, u32[]{:S(2)}) copy-start(f32[128]{0:T(128)} %copy-done.26) | copy-start | bytes 1540
  639.9 211.5 %all-gather.31.cloned.1.call-start = ((), (), s32[]{:S(2)}) async-start(), calls=%async_computation.10 | async-start | bytes 1671168 | tf_op jit(solution)/shard_map/all_gather | solution.py:155
  684.5 63.8 %copy-start.14 = (f32[256,384]{1,0:T(8,128)}, f32[256,384]{1,0:T(8,128)S(1)}, u32[]{:S(2)}) copy-start(f32[256,384]{1,0:T(8,128)S(1)} %convert_element_type.128) | copy-start | bytes 1179652
  684.7 63.6 %copy-start.12 = (f32[128,384]{1,0:T(8,128)}, f32[128,384]{1,0:T(8,128)S(1)}, u32[]{:S(2)}) copy-start(f32[128,384]{1,0:T(8,128)S(1)} %get-tuple-element.23) | copy-start | bytes 589828
  748.4 6.8 copy-start.18
  756.0 176.9 %all-gather.33.cloned.1.call-start = ((), (), s32[]{:S(2)}) async-start(), calls=%async_computation.11 | async-start | bytes 1671168 | tf_op jit(solution)/shard_map/all_gather | solution.py:157
  756.7 257.5 %all-gather.25.cloned.1.call-start = ((), (), s32[]{:S(2)}) async-start(), calls=%async_computation.7 | async-start | bytes 1671168 | tf_op jit(solution)/shard_map/all_gather | solution.py:156
  758.7 0.7 copy-start.22
  761.2 334.6 %all-gather.23.cloned.1.call-start = ((), (), s32[]{:S(2)}) async-start(), calls=%async_computation.6 | async-start | bytes 1671168 | tf_op jit(solution)/shard_map/all_gather | solution.py:154
  761.9 411.4 %reduce-scatter.9.cloned.1.call-start = ((), (), s32[]{:S(2)}) async-start(), calls=%async_computation.13 | async-start | bytes 1769472
  762.1 6.2 copy-start.9
  762.1 6.4 slice-start
  763.9 4.7 slice-start.1
  1102.3 4.7 copy-start.6
  1117.6 0.9 copy-start.10
  1117.6 0.9 copy-start.24
  1118.6 1.1 copy-start.16
  1119.7 1.2 copy-start.3
  1120.9 1.1 copy-start.7
  1122.1 2.1 copy-start.1
  1129.0 45.4 %copy-start.13 = (f32[128,384]{1,0:T(8,128)S(1)}, f32[128,384]{1,0:T(8,128)}, u32[]{:S(2)}) copy-start(f32[128,384]{1,0:T(8,128)} %copy-done.12) | copy-start | bytes 589828
  1129.0 45.4 %copy-start.23 = (f32[384]{0:T(512)S(1)}, f32[384]{0:T(512)}, u32[]{:S(2)}) copy-start(f32[384]{0:T(512)} %get-tuple-element.15) | copy-start | bytes 4612
Sparse Core Ops, SparseCore 0:
  85.7 94.2 all-gather.26
  182.6 78.8 all-gather.28
  264.7 78.8 all-gather.16
  346.0 78.8 all-gather.14
  427.4 100.9 all-gather.18
  530.8 100.4 all-gather.20
  640.0 43.3 reduce-scatter.6
  756.1 95.2 all-gather.30
  854.0 78.8 all-gather.32
  935.3 78.8 all-gather.24
  1016.8 78.8 all-gather.22
  1129.2 44.1 reduce-scatter.8
where the time goes:
time: 1220 us; the launch traced here: 1210 us
  waiting for transfers between devices  892 us (73%)
  blocking collectives  160 us (13%)
  local copies, waits for them, and re-layouts  76.3 us (6%)
  matrix products  42.8 us (4%)
  other arithmetic  27.4 us (2%)
  between operations  14.8 us (1%)
    all_gather x2, waiting for transfers between devices, local(): lax.all_gather(dv_rows, 'ctx', axis=0, tiled=True)  159 us
    all_gather x2, waiting for transfers between devices, local(): lax.all_gather(dk_rows, 'ctx', axis=0, tiled=True)  157 us
    all_gather x2, waiting for transfers between devices, local(): lax.all_gather(k_rows, 'ctx', axis=0, tiled=True)  157 us
    all_gather x2, waiting for transfers between devices, local(): lax.all_gather(v_rows, 'ctx', axis=0, tiled=True)  154 us
    all_gather x1, waiting for transfers between devices, local(): lax.all_gather(w_down, 'ctx', axis=1, tiled=True)  98.5 us
    unnamed x14, waiting for transfers between devices  90.1 us
    all_gather x1, waiting for transfers between devices, local(): lax.all_gather(w_up, 'ctx', axis=0, tiled=True)  76.6 us
    all_gather x2, blocking collectives, norm_features(): lax.all_gather(tangent_act, 'tp', axis=1, tiled=True)  49.3 us
  transfers between devices with their start and end apart: 12, of which 12 were waited for; matrix products, arithmetic and copies ran while one was open for 7% of the time, Pallas kernels for 0%

commit v1 on v0

v1 whole, which is shorter than its diff:
```python
from functools import partial
import math

import jax
import jax.numpy as jnp
from jax import lax
from jax.experimental import pallas as pl
from jax.experimental.pallas import tpu as pltpu
from jax.sharding import PartitionSpec as P

HD = 128
BLK = 128
K_SEL = 8
STEPS = 2
NTP = 8
NZ = 8
NCTX = 16
W = 384
HALF = 64
ROWS = 256

EPS = 1e-06
NEG_BIG = -1e30
MESH = pl.DeviceIdType.MESH
F32 = jnp.float32
BF16 = jnp.bfloat16


def place():
    ctx, tp, core = lax.axis_index("ctx"), lax.axis_index("tp"), lax.axis_index("probe")
    return ctx, tp, core


def tp_at(offset):
    ctx, tp, core = place()
    return (ctx, lax.rem(tp + offset + NTP, NTP), core)


def sibling():
    ctx, tp, core = place()
    return (ctx, tp, 1 - core)


def ctx_at(block):
    _, tp, core = place()
    return (block, tp, core)


def greet(devices):
    barrier = pltpu.get_barrier_semaphore()
    for device in devices:
        pl.semaphore_signal(barrier, inc=1, device_id=device, device_id_type=MESH)
    pl.semaphore_wait(barrier, len(devices))


def remote(src, dst, send_sem, recv_sem, device):
    return pltpu.make_async_remote_copy(
        src_ref=src,
        dst_ref=dst,
        send_sem=send_sem,
        recv_sem=recv_sem,
        device_id=device,
        device_id_type=MESH,
    )


def feature_cols(owner):
    return pl.ds(pl.multiple_of(owner * W, 128), W)


def norm_kernel(lat, tan, shift, stretch, out, stat, s_send, s_recv, x_send, x_recv, f_send, f_recv):
    _, tp, core = place()
    rows_sent = pl.ds(pl.multiple_of(core * HALF, HALF), 3 * HALF)
    full = float(W * NTP)
    greet([tp_at(i) for i in range(1, NTP)] + [sibling()])
    rows, tangent = lat[...], tan[...]
    sums = [
        jnp.sum(rows, 1, keepdims=True),
        jnp.sum(rows * rows, 1, keepdims=True),
        jnp.sum(tangent, 1, keepdims=True),
        jnp.sum(rows * tangent, 1, keepdims=True),
    ]
    lane = lax.broadcasted_iota(jnp.int32, (BLK, BLK), 1)
    packed = jnp.zeros((BLK, BLK), F32)
    for n, column in enumerate(sums):
        packed = jnp.where(lane == n, column, packed)
    stat[tp] = packed.T[0:8]
    copies = []
    for i in range(1, NTP):
        copy = remote(stat.at[tp], stat.at[tp], s_send.at[i], s_recv.at[i], tp_at(i))
        copy.start()
        copies.append(copy)
    for i in range(1, NTP):
        source = lax.rem(tp - i + NTP, NTP)
        remote(stat.at[source], stat.at[source], s_send.at[i], s_recv.at[i], tp_at(i)).wait_recv()
    total = stat[0]
    for n in range(1, NTP):
        total = total + stat[n]
    total = jnp.concatenate([total, jnp.zeros((BLK - 8, BLK), F32)], axis=0).T * (1.0 / full)
    row_mean, row_sq, tan_mean, tan_sq = (total[:, n : n + 1] for n in range(4))
    row_var = row_sq - row_mean * row_mean
    tan_var = 2.0 * (tan_sq - row_mean * tan_mean)
    inv_std = lax.rsqrt(row_var + EPS)
    centred = rows - row_mean
    gain = 1.0 + stretch[...]
    normed = (centred * inv_std * gain + shift[...]).astype(BF16)
    tan_normed = (tangent - tan_mean) * inv_std - 0.5 * centred * (
        inv_std * inv_std * inv_std * tan_var
    )
    mine = feature_cols(tp)
    out[0:HALF, mine] = normed[0:HALF]
    out[HALF : 3 * HALF, mine] = (tan_normed * gain).astype(BF16)
    out[3 * HALF : ROWS, mine] = normed[HALF:BLK]
    for i in range(1, NTP):
        copy = remote(
            out.at[rows_sent, mine], out.at[rows_sent, mine], x_send.at[i], x_recv.at[i], tp_at(i)
        )
        copy.start()
        copies.append(copy)
    shared = pl.ds(pl.multiple_of(core * 3 * HALF, HALF), HALF)
    other = pl.ds(pl.multiple_of((1 - core) * 3 * HALF, HALF), HALF)
    for i in range(1, NTP):
        cols = feature_cols(lax.rem(tp - i + NTP, NTP))
        here = out.at[rows_sent, cols]
        remote(here, here, x_send.at[i], x_recv.at[i], tp_at(i)).wait_recv()
        piece = out.at[shared, cols]
        copy = remote(piece, piece, f_send.at[i], f_recv.at[i], sibling())
        copy.start()
        copies.append(copy)
    for i in range(1, NTP):
        cols = feature_cols(lax.rem(tp - i + NTP, NTP))
        piece = out.at[other, cols]
        remote(piece, piece, f_send.at[i], f_recv.at[i], sibling()).wait_recv()
    for copy in copies:
        copy.wait_send()


def norm_gather(lat, tan, shift, stretch):
    sems = [pltpu.SemaphoreType.DMA((NTP,)) for _ in range(6)]
    return pl.pallas_call(
        norm_kernel,
        out_shape=jax.ShapeDtypeStruct((ROWS, W * NTP), BF16),
        in_specs=[pl.BlockSpec(memory_space=pltpu.VMEM)] * 4,
        out_specs=pl.BlockSpec(memory_space=pltpu.VMEM),
        scratch_shapes=[pltpu.VMEM((NTP, 8, BLK), F32)] + sems,
        compiler_params=pltpu.CompilerParams(collective_id=1, has_side_effects=True),
        name="norm_gather",
    )(lat, tan, shift, stretch)


def ring_devices():
    ctx, _, _ = place()
    z, h = lax.rem(ctx, NZ), lax.div(ctx, NZ)
    right = h * NZ + lax.rem(z + 1, NZ)
    left = h * NZ + lax.rem(z + NZ - 1, NZ)
    across = (1 - h) * NZ + z
    return ctx_at(right), ctx_at(left), ctx_at(across)


def ring_gather(own, passed, given, sems):
    send, recv, f_send, f_recv = sems
    ctx, _, _ = place()
    z, h = lax.rem(ctx, NZ), lax.div(ctx, NZ)
    right, left, across = ring_devices()
    copies = []

    def push(block, n, device):
        copy = remote(own(block), own(block), send.at[n], recv.at[n], device)
        copy.start()
        copies.append(copy)

    def arrive(block, n):
        remote(own(block), own(block), send.at[n], recv.at[n], across).wait_recv()
        copy = remote(passed(block), passed(block), f_send.at[n], f_recv.at[n], sibling())
        copy.start()
        copies.append(copy)

    def at(row, step):
        return row * NZ + lax.rem(z + step + NZ, NZ)

    push(ctx, 0, across)
    push(ctx, 1, right)
    push(ctx, 8, left)
    arrive(at(1 - h, 0), 0)
    push(at(1 - h, 0), 5, right)
    push(at(1 - h, 0), 11, left)
    taken = [(at(1 - h, 0), 0)]
    for s in range(1, 5):
        for row, step, base, reach, device in (
            (h, -s, 0, 4, right),
            (h, s, 7, 3, left),
            (1 - h, -s, 4, 3, right),
            (1 - h, s, 10, 4, left),
        ):
            if s <= reach:
                block = at(row, step)
                arrive(block, base + s)
                taken.append((block, base + s))
                if s < reach:
                    push(block, base + s + 1, device)
    for block, n in taken:
        remote(given(block), given(block), f_send.at[n], f_recv.at[n], sibling()).wait_recv()
    for copy in copies:
        copy.wait_send()


def ring_sems():
    return [pltpu.SemaphoreType.DMA((15,)) for _ in range(4)]


def kv_kernel(mine, out, *sems):
    ctx, _, core = place()
    right, left, across = ring_devices()
    greet([right, left, across, sibling()])
    out[ctx] = mine[...]
    ring_gather(
        lambda block: out.at[block, pl.ds(core, 3)],
        lambda block: out.at[block, pl.ds(core * 3, 1)],
        lambda block: out.at[block, pl.ds((1 - core) * 3, 1)],
        sems,
    )


def kv_gather(mine):
    return pl.pallas_call(
        kv_kernel,
        out_shape=jax.ShapeDtypeStruct((NCTX,) + mine.shape, mine.dtype),
        in_specs=[pl.BlockSpec(memory_space=pltpu.VMEM)],
        out_specs=pl.BlockSpec(memory_space=pltpu.VMEM),
        scratch_shapes=ring_sems(),
        compiler_params=pltpu.CompilerParams(collective_id=2, has_side_effects=True),
        name="kv_gather",
    )(mine)


def weight_kernel(mine, out, *sems):
    ctx, _, core = place()
    right, left, across = ring_devices()
    greet([right, left, across, sibling()])
    out[0, ctx] = mine[0]
    out[1, ctx] = mine[1]
    ring_gather(
        lambda block: out.at[core, block],
        lambda block: out.at[core, block],
        lambda block: out.at[1 - core, block],
        sems,
    )


def weight_gather(mine):
    return pl.pallas_call(
        weight_kernel,
        out_shape=jax.ShapeDtypeStruct((2, NCTX) + mine.shape[1:], mine.dtype),
        in_specs=[pl.BlockSpec(memory_space=pltpu.VMEM)],
        out_specs=pl.BlockSpec(memory_space=pltpu.VMEM),
        scratch_shapes=ring_sems(),
        compiler_params=pltpu.CompilerParams(collective_id=3, has_side_effects=True),
        name="weight_gather",
    )(mine)


def reduce_kernel(part, out, got, r_send, r_recv, p_sem):
    _, tp, core = place()
    rows_sent = pl.ds(pl.multiple_of(core * HALF, HALF), 3 * HALF)
    greet([tp_at(i) for i in range(1, NTP)] + [sibling()])
    copies = []
    for i in range(1, NTP):
        cols = feature_cols(lax.rem(tp + i, NTP))
        copy = remote(part.at[rows_sent, cols], got.at[i], r_send.at[i], r_recv.at[i], tp_at(i))
        copy.start()
        copies.append(copy)
    total = part[rows_sent, feature_cols(tp)].astype(F32)
    for i in range(1, NTP):
        remote(got.at[i], got.at[i], r_send.at[i], r_recv.at[i], tp_at(i)).wait_recv()
        total = total + got[i].astype(F32)
    out[rows_sent] = total
    piece = out.at[pl.ds(pl.multiple_of(core * 3 * HALF, HALF), HALF)]
    other = out.at[pl.ds(pl.multiple_of((1 - core) * 3 * HALF, HALF), HALF)]
    copy = remote(piece, piece, p_sem.at[0], p_sem.at[1], sibling())
    copy.start()
    remote(other, other, p_sem.at[0], p_sem.at[1], sibling()).wait_recv()
    copies.append(copy)
    for copy in copies:
        copy.wait_send()


def reduce_parts(part):
    return pl.pallas_call(
        reduce_kernel,
        out_shape=jax.ShapeDtypeStruct((ROWS, W), F32),
        in_specs=[pl.BlockSpec(memory_space=pltpu.VMEM)],
        out_specs=pl.BlockSpec(memory_space=pltpu.VMEM),
        scratch_shapes=[
            pltpu.VMEM((NTP, 3 * HALF, W), BF16),
            pltpu.SemaphoreType.DMA((NTP,)),
            pltpu.SemaphoreType.DMA((NTP,)),
            pltpu.SemaphoreType.DMA((2,)),
        ],
        compiler_params=pltpu.CompilerParams(collective_id=4, has_side_effects=True),
        name="reduce_parts",
    )(part)


def primal_rows(rows):
    return jnp.concatenate([rows[0:HALF], rows[3 * HALF : ROWS]], axis=0)


def tangent_rows(rows):
    return rows[HALF : 3 * HALF]


def mixed_rows(primal, tangent):
    return jnp.concatenate([primal[0:HALF], tangent, primal[HALF:BLK]], axis=0)


def head_rms(projected, tan_projected, head_gain):
    row_count = projected.shape[0]
    heads_local = head_gain.shape[0] // HD
    head_view = projected.reshape(row_count, heads_local, HD)
    tan_view = tan_projected.reshape(row_count, heads_local, HD)
    gain_view = head_gain.reshape(heads_local, HD)
    inv_std = lax.rsqrt(jnp.mean(head_view * head_view, axis=-1, keepdims=True) + EPS)
    tan_inv = -inv_std * inv_std * inv_std * jnp.mean(head_view * tan_view, axis=-1, keepdims=True)
    result = (head_view * inv_std * gain_view).astype(BF16)
    tan_result = ((tan_view * inv_std + head_view * tan_inv) * gain_view).astype(BF16)
    return (result, tan_result)


def attend(query, kv, pattern):
    q_rows, dq_rows = query
    chosen = pattern[0]
    valid = (jnp.arange(K_SEL) == 0) | (chosen != chosen[0])
    key_mask = jnp.repeat(valid, BLK)[None, None, :]
    listed = jnp.take(kv, chosen, axis=0)

    def member(n):
        return listed[:, n].reshape(K_SEL * BLK, W // HD, HD)

    k_rows, dk_rows, dv_rows, v_rows = (member(n) for n in range(4))
    scale = 1.0 / math.sqrt(HD)
    dot = partial(jnp.einsum, preferred_element_type=F32)
    scores = dot("qhd,khd->hqk", q_rows, k_rows) * scale
    tan_scores = (
        dot("qhd,khd->hqk", dq_rows, k_rows) + dot("qhd,khd->hqk", q_rows, dk_rows)
    ) * scale
    scores = jnp.where(key_mask, scores, NEG_BIG)
    weights = jnp.where(key_mask, jnp.exp(scores - jnp.max(scores, 2, keepdims=True)), 0.0)
    weighted = weights * tan_scores
    total = jnp.sum(weights, 2)[:, :, None]
    tan_total = jnp.sum(weighted, 2)[:, :, None]
    weights, weighted = weights.astype(BF16), weighted.astype(BF16)
    output = dot("hqk,khd->hqd", weights, v_rows) / total
    tan_output = (
        dot("hqk,khd->hqd", weights, dv_rows) + dot("hqk,khd->hqd", weighted, v_rows)
    ) / total - (tan_total / total) * output

    def flat(rows):
        return rows.transpose(1, 0, 2).reshape(BLK, W).astype(BF16)

    return flat(output), flat(tan_output)


def local(latent, probes, modulation, pattern, w_qkv, w_out, w_up, w_down, q_gain, k_gain):
    row_count, local_width = latent.shape
    full_width = local_width * lax.axis_size("tp")
    feature_start = lax.axis_index("tp") * local_width
    step_size = 1.0 / STEPS
    signs = 2.0 * probes[0].astype(F32) - 1.0
    weights = weight_gather(jnp.stack([w_up, w_down.T]))
    up_full = weights[0].reshape(full_width, -1)
    down_full = weights[1].reshape(full_width, -1)
    gelu_tanh = partial(jax.nn.gelu, approximate=True)
    change = jnp.zeros((row_count,), F32)
    for euler_step in range(STEPS):
        mod_local = lax.dynamic_slice_in_dim(modulation[euler_step], feature_start, local_width, 1)
        stacked = norm_gather(latent, signs, mod_local[0:1], mod_local[1:2])
        projected = jnp.einsum("rd,dcf->crf", stacked, w_qkv, preferred_element_type=F32)
        q_rows, dq_rows = head_rms(primal_rows(projected[0]), tangent_rows(projected[0]), q_gain)
        k_rows, dk_rows = head_rms(primal_rows(projected[1]), tangent_rows(projected[1]), k_gain)
        v_rows = primal_rows(projected[2]).astype(BF16)
        dv_rows = tangent_rows(projected[2]).astype(BF16)
        kv = kv_gather(
            jnp.stack([k_rows.reshape(BLK, W), dk_rows.reshape(BLK, W), dv_rows, v_rows])
        )
        attended, tan_attended = attend((q_rows, dq_rows), kv, pattern)
        pre_hidden = jnp.dot(stacked, up_full, preferred_element_type=F32)
        hidden, tan_hidden = jax.jvp(
            gelu_tanh, (primal_rows(pre_hidden),), (tangent_rows(pre_hidden),)
        )
        attn_rows = mixed_rows(attended, tan_attended)
        mlp_rows = mixed_rows(hidden.astype(BF16), tan_hidden.astype(BF16))
        parts = jnp.dot(attn_rows, w_out, preferred_element_type=F32) + jnp.einsum(
            "rf,df->rd", mlp_rows, down_full, preferred_element_type=F32
        )
        summed = reduce_parts(parts.astype(BF16))
        speed = mod_local[2] * primal_rows(summed)
        tan_speed = mod_local[2] * tangent_rows(summed)
        change = change + jnp.sum(signs * tan_speed, axis=1)
        latent = latent + step_size * speed
    total_change = lax.psum(change, ("tp", "probe"))
    density_change = -step_size * total_change / (lax.axis_size("probe") * math.sqrt(full_width))
    return (latent, density_change)


def solution(mesh):
    return jax.shard_map(
        local,
        mesh=mesh,
        in_specs=(
            P("ctx", "tp"),
            P("probe", "ctx", "tp"),
            P(),
            P("ctx", None),
            P(None, None, "tp"),
            P("tp", None),
            P("ctx", "tp"),
            P("tp", "ctx"),
            P("tp"),
            P("tp"),
        ),
        out_specs=(P("ctx", "tp"), P("ctx")),
        check_vma=False,
    )
```

time: 1220 us -> 465 us (0.38)
  waiting for transfers between devices: 892 us -> 0 us
  Pallas kernels: 0 us -> 279 us
  blocking collectives: 160 us -> 26.7 us
  matrix products: 42.8 us -> 67.9 us
  local copies, waits for them, and re-layouts: 76.3 us -> 62.6 us
  between operations: 14.8 us -> 1.35 us
    all_gather x10 -> x0, waiting for transfers between devices: 802 us -> none  [the longest x2 159 us: local(): lax.all_gather(dv_rows, 'ctx', axis=0, tiled=True)]
    pallas_call x0 -> x7, Pallas kernels: none -> 279 us  [the longest x2 120 us: kv_gather(): pl.pallas_call(kv_kernel, out_shape=jax.ShapeDtypeStruct((NCTX,) + mine.s...]
    all_gather x4 -> x0, blocking collectives: 98.3 us -> none  [the longest x2 49.3 us: norm_features(): lax.all_gather(tangent_act, 'tp', axis=1, tiled=True)]
    unnamed x14 -> x0, waiting for transfers between devices: 90.1 us -> none
    psum x2 -> x0, blocking collectives: 31.4 us -> none  [norm_features(): totals = lax.psum(row_sums, 'tp')]
    slice x6 -> x34, local copies, waits for them, and re-layouts: 4.8 us -> 32.1 us  [the longest x8 14.2 us: member(): return listed[:, n].reshape(K_SEL * BLK, W // HD, HD)]
    dot_general x20, matrix products: 42.8 us -> 64.3 us  [the longest x2 11.2 us: local(): jnp.einsum('rd,dcf->crf', stacked, w_qkv, preferred_element_type=F32)]
    reshape x8 -> x4, local copies, waits for them, and re-layouts: 17.1 us -> 0.57 us  [head_rms(): tan_view = tan_projected.reshape(row_count, heads_local, HD)]
  transfers between devices with their start and end apart: 12 -> 0, of which waited for: 12 -> 0; matrix products, arithmetic and copies ran while one was open for 7% -> 0% of each run, Pallas kernels for 0% -> 0%
where the time goes in v1:
time: 465 us; the launch traced here: 462 us
  Pallas kernels  279 us (60%)
  matrix products  67.9 us (15%)
  local copies, waits for them, and re-layouts  62.6 us (13%)
  blocking collectives  26.7 us (6%)
  other arithmetic  25 us (5%)
    pallas_call x2, Pallas kernels, kv_gather(): pl.pallas_call(kv_kernel, out_shape=jax.ShapeDtypeStruct((NCTX,) + mine.s...  120 us
    pallas_call x1, Pallas kernels, weight_gather(): pl.pallas_call(weight_kernel, out_shape=jax.ShapeDtypeStruct((2, NCTX) +...  59 us
    pallas_call x2, Pallas kernels, norm_gather(): pl.pallas_call(norm_kernel, out_shape=jax.ShapeDtypeStruct((ROWS, W * NTP...  57.8 us
    pallas_call x2, Pallas kernels, reduce_parts(): pl.pallas_call(reduce_kernel, out_shape=jax.ShapeDtypeStruct((ROWS, W), F...  42.2 us
    psum x1, blocking collectives, local(): total_change = lax.psum(change, ('tp', 'probe'))  26.7 us
    slice x8, local copies, waits for them, and re-layouts, member(): return listed[:, n].reshape(K_SEL * BLK, W // HD, HD)  14.2 us
    another operation x8, local copies, waits for them, and re-layouts, member(): return listed[:, n].reshape(K_SEL * BLK, W // HD, HD)  12.3 us
    dot_general x2, matrix products, local(): jnp.einsum('rd,dcf->crf', stacked, w_qkv, preferred_element_type=F32)  11.2 us

profile of v1, /device:TPU:1, one launch (start us, length us, event | category | flops | bytes accessed | tf_op | source)
XLA Modules:
  0.0 462.5 jit_solution(14246773797297298562)
XLA Ops:
  1.5 1.8 compare_or_fusion
  6.7 1.6 add_bitcast_fusion.tan
  8.3 1.9 pad_maximum_fusion.mine
  10.2 27.2 %norm_gather.2 = bf16[256,3072]{1,0:T(8,128)(2,1)} custom-call(f32[128,384]{1,0:T(8,128)} %lat.1, f32[128,384]{1,0:T(8,128)} %add_bitcast_fusion.tan, f32[1,384]{1,0:T(1,128)} %get-tuple-element.97.shift, f32[1,384]{1,0:T(1,128)} %get-tuple-element.96.stretch), custom_call_target="tpu_custom_call" | custom-call | tf_op jit(solution)/shard_map/norm_gather/pallas_call | solution.py:140
  37.5 5.7 %fusion.134 = (bf16[3,256,384]{2,1,0:T(8,128)(2,1)S(1)}, f32[3,256,384]{2,1,0:T(8,128)S(1)}) fusion(bf16[3072,3,384]{2,0,1:T(8,128)(2,1)} %param.16, bf16[256,3072]{1,0:T(8,128)(2,1)} %norm_gather.2), kind=kOutput, calls=%fused_computation.210 | convolution fusion | flops 1812234240 | bytes 10420224 | tf_op jit(solution)/shard_map/rd,dcf->crf/dot_general | solution.py:377
  48.6 1.8 fusion.121
  53.2 1.6 maximum_maximum_fusion.mine
  54.9 61.6 %kv_gather.2 = bf16[16,4,128,384]{3,2,1,0:T(8,128)(2,1)} custom-call(bf16[4,128,384]{2,1,0:T(8,128)(2,1)} %maximum_maximum_fusion.mine), custom_call_target="tpu_custom_call" | custom-call | tf_op jit(solution)/shard_map/kv_gather/pallas_call | solution.py:225
  116.5 5.6 %gather_fusion = bf16[8,4,128,384]{3,2,1,0:T(8,128)(2,1)} fusion(bf16[16,4,128,384]{3,2,1,0:T(8,128)(2,1)} %kv_gather.2, s32[1024]{0:T(1024)} %pad_clamp_fusion), kind=kCustom, calls=%fused_computation.clone | custom fusion | bytes 6291488 | tf_op jit(solution)/shard_map/jit(_take)/gather | solution.py:334
  122.1 2.3 broadcast_select_fusion.1
  124.4 1.6 fusion.118
  127.1 1.6 copy.160
  129.9 2.5 copy.157
  132.5 2.2 reshape_squeeze.31
  136.0 1.6 reshape_squeeze.30
  137.6 2.3 fusion.88
  141.5 3.3 fusion.71
  144.8 1.8 fusion.135
  146.6 3.6 fusion.137
  150.1 3.0 fusion.136
  153.2 1.7 fusion.25
  155.3 59.0 %weight_gather.1 = bf16[2,16,192,768]{3,2,1,0:T(8,128)(2,1)} custom-call(bf16[2,192,768]{2,1,0:T(8,128)(2,1)} %pad_maximum_fusion.mine), custom_call_target="tpu_custom_call" | custom-call | tf_op jit(solution)/shard_map/weight_gather/pallas_call | solution.py:251
  214.3 6.9 %fusion.116 = (bf16[1,16,192,768]{3,2,1,0:T(8,128)(2,1)}, bf16[1,16,192,768]{3,2,1,0:T(8,128)(2,1)S(1)}) fusion(bf16[2,16,192,768]{3,2,1,0:T(8,128)(2,1)} %weight_gather.1), kind=kLoop, calls=%fused_computation.192 | loop fusion | bytes 18874368 | tf_op jit(solution)/shard_map/slice | solution.py:370
  221.2 5.4 %fusion.142 = f32[256,768]{1,0:T(8,128)S(1)} fusion(bf16[256,3072]{1,0:T(8,128)(2,1)S(1)} %copy-done.5, bf16[3072,768]{1,0:T(8,128)(2,1)} %bitcast.158), kind=kOutput, calls=%fused_computation.218 | convolution fusion | flops 1207959552 | bytes 7077888 | tf_op jit(solution)/shard_map/dot_general | solution.py:386
  228.5 2.3 fusion.2.part
  230.7 20.8 %reduce_parts.2 = f32[256,384]{1,0:T(8,128)} custom-call(bf16[256,3072]{1,0:T(8,128)(2,1)} %fusion.2.part), custom_call_target="tpu_custom_call" | custom-call | tf_op jit(solution)/shard_map/reduce_parts/pallas_call | solution.py:288
  253.2 30.6 %norm_gather.3 = bf16[256,3072]{1,0:T(8,128)(2,1)} custom-call(f32[128,384]{1,0:T(8,128)} %fusion.80.lat, f32[128,384]{1,0:T(8,128)} %add_bitcast_fusion.tan, f32[1,384]{1,0:T(1,128)} %get-tuple-element.64.shift, f32[1,384]{1,0:T(1,128)} %get-tuple-element.65.stretch), custom_call_target="tpu_custom_call" | custom-call | tf_op jit(solution)/shard_map/norm_gather/pallas_call | solution.py:140
  283.9 5.2 %fusion.143 = f32[256,768]{1,0:T(8,128)} fusion(bf16[256,3072]{1,0:T(8,128)(2,1)} %norm_gather.3, bf16[3072,768]{1,0:T(8,128)(2,1)} %bitcast.159), kind=kOutput, calls=%fused_computation.219 | convolution fusion | flops 1207959552 | bytes 7077888 | tf_op jit(solution)/shard_map/dot_general | solution.py:386
  289.1 5.5 %fusion.138 = (bf16[3,256,384]{2,1,0:T(8,128)(2,1)S(1)}, f32[3,256,384]{2,1,0:T(8,128)S(1)}) fusion(bf16[3072,3,384]{2,0,1:T(8,128)(2,1)} %param.16, bf16[256,3072]{1,0:T(8,128)(2,1)S(1)} %copy-done.6), kind=kOutput, calls=%fused_computation.214 | convolution fusion | flops 1812234240 | bytes 10420224 | tf_op jit(solution)/shard_map/rd,dcf->crf/dot_general | solution.py:377
  300.0 1.8 fusion.119
  304.0 1.6 maximum_maximum_fusion.1.mine
  306.0 5.5 %fusion.62 = f32[256,3072]{1,0:T(8,128)} fusion(bf16[3072,768]{1,0:T(8,128)(2,1)} %bitcast.157, bf16[64,768]{1,0:T(8,128)(2,1)S(1)} %get-tuple-element.54, bf16[128,768]{1,0:T(8,128)(2,1)S(1)} %get-tuple-element.47, bf16[64,768]{1,0:T(8,128)(2,1)S(1)} %get-tuple-element.53), kind=kOutput, calls=%fused_computation.83 | convolution fusion | flops 1209139200 | bytes 8257536 | tf_op jit(solution)/shard_map/rf,df->rd/dot_general | solution.py:392
  311.4 58.3 %kv_gather.3 = bf16[16,4,128,384]{3,2,1,0:T(8,128)(2,1)} custom-call(bf16[4,128,384]{2,1,0:T(8,128)(2,1)} %maximum_maximum_fusion.1.mine), custom_call_target="tpu_custom_call" | custom-call | tf_op jit(solution)/shard_map/kv_gather/pallas_call | solution.py:225
  369.7 5.5 %gather_fusion.1 = bf16[8,4,128,384]{3,2,1,0:T(8,128)(2,1)} fusion(bf16[16,4,128,384]{3,2,1,0:T(8,128)(2,1)} %kv_gather.3, s32[1024]{0:T(1024)} %pad_clamp_fusion), kind=kCustom, calls=%fused_computation.1.clone | custom fusion | bytes 6291488 | tf_op jit(solution)/shard_map/jit(_take)/gather | solution.py:334
  375.3 2.3 broadcast_select_fusion
  377.6 1.6 fusion.117
  380.3 1.6 copy.187
  383.1 2.5 copy.184
  385.7 2.1 reshape_squeeze.37
  389.2 1.7 reshape_squeeze.36
  394.0 2.6 fusion.68
  396.7 1.8 fusion.139
  398.5 3.6 fusion.141
  402.0 3.1 fusion.140
  407.0 4.1 fusion.3.part
  411.2 21.4 %reduce_parts.3 = f32[256,384]{1,0:T(8,128)} custom-call(bf16[256,3072]{1,0:T(8,128)(2,1)} %fusion.3.part), custom_call_target="tpu_custom_call" | custom-call | tf_op jit(solution)/shard_map/reduce_parts/pallas_call | solution.py:288
  433.6 1.7 multiply_reduce_fusion.4
  435.3 26.7 %psum.7 = f32[128]{0:T(128)S(1)} all-reduce(f32[128]{0:T(128)S(1)} %add.149), channel_id=1, replica_groups=mesh['ctx'=16,'tp'=8,'probe'=2] {'tp','probe'}, use_global_device_ids=true, to_apply=%region_16.18 | all-reduce | flops 128 | bytes 1024 | tf_op jit(solution)/shard_map/psum | solution.py:400
  (159 shorter events, 39.5 us)
Async XLA Ops:
  0.6 227.8 %copy-start = (bf16[384,3072]{1,0:T(8,128)(2,1)S(1)}, bf16[384,3072]{1,0:T(8,128)(2,1)}, u32[]{:S(2)}) copy-start(bf16[384,3072]{1,0:T(8,128)(2,1)} %param.17) | copy-start | bytes 7077892
  43.2 1.4 copy-start.13
  46.0 2.6 copy-start.26
  48.4 4.0 copy-start.25
  48.5 4.8 %copy-start.19 = (bf16[1,128,384]{2,1,0:T(8,128)(2,1)S(1)}, bf16[1,128,384]{2,1,0:T(8,128)(2,1)}, u32[]{:S(2)}) copy-start(bf16[1,128,384]{2,1,0:T(8,128)(2,1)} %slice.329) | copy-start | bytes 294916
  50.4 2.8 copy-start.21
  50.4 2.8 copy-start.22
  116.4 5.6 %copy-start.28 = (pred[8]{0:T(512)(128)(4,1)S(1)}, pred[8]{0:T(512)(128)(4,1)}, u32[]{:S(2)}) copy-start(pred[8]{0:T(512)(128)(4,1)} %get-tuple-element.79) | copy-start | bytes 28
  129.9 4.7 %copy-start.2 = (bf16[8,1,128,384]{3,2,1,0:T(8,128)(2,1)S(1)}, bf16[8,1,128,384]{3,2,1,0:T(8,128)(2,1)}, u32[]{:S(2)}) copy-start(bf16[8,1,128,384]{3,2,1,0:T(8,128)(2,1)} %get-tuple-element.22) | copy-start | bytes 2359300
  137.6 2.3 copy-start.10
  137.6 2.3 copy-start.30
  139.9 1.5 copy-start.31
  141.5 3.3 copy-start.11
  146.5 3.6 copy-start.15
  214.3 7.0 %copy-start.5 = (bf16[256,3072]{1,0:T(8,128)(2,1)S(1)}, bf16[256,3072]{1,0:T(8,128)(2,1)}, u32[]{:S(2)}) copy-start(bf16[256,3072]{1,0:T(8,128)(2,1)} %norm_gather.2) | copy-start | bytes 4718596
  221.2 5.8 %copy-start.1 = (bf16[1,16,192,768]{3,2,1,0:T(8,128)(2,1)}, bf16[1,16,192,768]{3,2,1,0:T(8,128)(2,1)S(1)}, u32[]{:S(2)}) copy-start(bf16[1,16,192,768]{3,2,1,0:T(8,128)(2,1)S(1)} %get-tuple-element.14) | copy-start | bytes 14155780
  230.7 21.8 %copy-start.16 = (f32[128,384]{1,0:T(8,128)S(1)}, f32[128,384]{1,0:T(8,128)}, u32[]{:S(2)}) copy-start(f32[128,384]{1,0:T(8,128)} %lat.1) | copy-start | bytes 589828
  283.9 5.2 %copy-start.6 = (bf16[256,3072]{1,0:T(8,128)(2,1)S(1)}, bf16[256,3072]{1,0:T(8,128)(2,1)}, u32[]{:S(2)}) copy-start(bf16[256,3072]{1,0:T(8,128)(2,1)} %norm_gather.3) | copy-start | bytes 4718596
  294.6 1.3 copy-start.12
  299.8 4.2 copy-start.20
  301.8 2.2 copy-start.23
  301.8 2.2 copy-start.24
  303.0 2.6 copy-start.17
  369.7 5.5 %copy-start.29 = (pred[8]{0:T(512)(128)(4,1)S(1)}, pred[8]{0:T(512)(128)(4,1)}, u32[]{:S(2)}) copy-start(pred[8]{0:T(512)(128)(4,1)} %get-tuple-element.79) | copy-start | bytes 28
  383.1 4.7 %copy-start.3 = (bf16[8,1,128,384]{3,2,1,0:T(8,128)(2,1)S(1)}, bf16[8,1,128,384]{3,2,1,0:T(8,128)(2,1)}, u32[]{:S(2)}) copy-start(bf16[8,1,128,384]{3,2,1,0:T(8,128)(2,1)} %get-tuple-element.18) | copy-start | bytes 2359300
  390.9 1.6 copy-start.8
  390.9 1.6 copy-start.32
  392.5 1.6 copy-start.33
  394.0 2.6 copy-start.9
  398.5 3.6 copy-start.14
  411.2 22.3 %copy-start.4 = (f32[128,384]{1,0:T(8,128)S(1)}, f32[128,384]{1,0:T(8,128)}, u32[]{:S(2)}) copy-start(f32[128,384]{1,0:T(8,128)} %fusion.80.lat) | copy-start | bytes 589828
  411.2 22.4 %copy-start.7 = (f32[256,384]{1,0:T(8,128)S(1)}, f32[256,384]{1,0:T(8,128)}, u32[]{:S(2)}) copy-start(f32[256,384]{1,0:T(8,128)} %reduce_parts.2) | copy-start | bytes 1179652
  411.2 22.4 %copy-start.18 = (s32[1,128,384]{2,1,0:T(8,128)S(1)}, s32[1,128,384]{2,1,0:T(8,128)}, u32[]{:S(2)}) copy-start(s32[1,128,384]{2,1,0:T(8,128)} %param.13) | copy-start | bytes 589828
  411.2 22.4 %copy-start.27 = (f32[384]{0:T(512)S(1)}, f32[384]{0:T(512)}, u32[]{:S(2)}) copy-start(f32[384]{0:T(512)} %get-tuple-element.63) | copy-start | bytes 4612

commit v2 on v0

v2 whole, which is shorter than its diff:
```python
from functools import partial
import math

import jax
import jax.numpy as jnp
from jax import lax
from jax.experimental import pallas as pl
from jax.experimental.pallas import tpu as pltpu
from jax.sharding import PartitionSpec as P

HD = 128
BLK = 128
K_SEL = 8
STEPS = 2
NTP = 8
NZ = 8
NCTX = 16
W = 384
D = 3072
HEADS = 3
UNITS = 768
SHARD = 192
HALF = 64
ROWS = 256

EPS = 1e-06
NEG_BIG = -1e30
MESH = pl.DeviceIdType.MESH
F32 = jnp.float32
BF16 = jnp.bfloat16


def place():
    return lax.axis_index("ctx"), lax.axis_index("tp"), lax.axis_index("probe")


def tp_at(offset):
    ctx, tp, core = place()
    return (ctx, lax.rem(tp + offset + NTP, NTP), core)


def sibling():
    ctx, tp, core = place()
    return (ctx, tp, 1 - core)


def ctx_at(block):
    _, tp, core = place()
    return (block, tp, core)


def ring_devices():
    ctx, _, _ = place()
    z, h = lax.rem(ctx, NZ), lax.div(ctx, NZ)
    right = h * NZ + lax.rem(z + 1, NZ)
    left = h * NZ + lax.rem(z + NZ - 1, NZ)
    across = (1 - h) * NZ + z
    return ctx_at(right), ctx_at(left), ctx_at(across)


def greet(devices):
    barrier = pltpu.get_barrier_semaphore()
    for device in devices:
        pl.semaphore_signal(barrier, inc=1, device_id=device, device_id_type=MESH)
    pl.semaphore_wait(barrier, len(devices))


def remote(src, dst, send_sem, recv_sem, device):
    return pltpu.make_async_remote_copy(
        src_ref=src,
        dst_ref=dst,
        send_sem=send_sem,
        recv_sem=recv_sem,
        device_id=device,
        device_id_type=MESH,
    )


def feature_cols(owner):
    return pl.ds(pl.multiple_of(owner * W, 128), W)


def half_rows(core):
    return pl.ds(pl.multiple_of(core * 3 * HALF, HALF), HALF)


class Ring:
    def __init__(self, own, passed, given, sems):
        self.own, self.passed, self.given = own, passed, given
        self.send, self.recv, self.f_send, self.f_recv = sems
        ctx, _, _ = place()
        z, h = lax.rem(ctx, NZ), lax.div(ctx, NZ)
        self.ctx = ctx
        self.right, self.left, self.across = ring_devices()
        self.copies, self.taken = [], []

        def at(row, step):
            return row * NZ + lax.rem(z + step + NZ, NZ)

        self.beside = at(1 - h, 0)
        self.todo = [(self.beside, 0, ((5, self.right), (11, self.left)))]
        for s in range(1, 5):
            for row, step, base, reach, device in (
                (h, -s, 0, 4, self.right),
                (h, s, 7, 3, self.left),
                (1 - h, -s, 4, 3, self.right),
                (1 - h, s, 10, 4, self.left),
            ):
                if s <= reach:
                    onward = ((base + s + 1, device),) if s < reach else ()
                    self.todo.append((at(row, step), base + s, onward))

    def push(self, block, n, device):
        copy = remote(self.own(block), self.own(block), self.send.at[n], self.recv.at[n], device)
        copy.start()
        self.copies.append(copy)

    def start(self):
        self.push(self.ctx, 0, self.across)
        self.push(self.ctx, 1, self.right)
        self.push(self.ctx, 8, self.left)

    def advance(self, count=1):
        for _ in range(count):
            if not self.todo:
                return
            block, n, onward = self.todo.pop(0)
            mine = self.own(block)
            remote(mine, mine, self.send.at[n], self.recv.at[n], self.across).wait_recv()
            for later, device in onward:
                self.push(block, later, device)
            piece = self.passed(block)
            copy = remote(piece, piece, self.f_send.at[n], self.f_recv.at[n], sibling())
            copy.start()
            self.copies.append(copy)
            self.taken.append((block, n))

    def finish(self):
        self.advance(len(self.todo))
        for block, n in self.taken:
            piece = self.given(block)
            remote(piece, piece, self.f_send.at[n], self.f_recv.at[n], sibling()).wait_recv()

    def drain(self):
        for copy in self.copies:
            copy.wait_send()


def gelu_pair(pre, tan_pre):
    c = math.sqrt(2.0 / math.pi)
    square = pre * pre
    t = jnp.tanh(c * (pre + 0.044715 * (square * pre)))
    half = 0.5 * (1.0 + t)
    slope = half + 0.5 * pre * (1.0 - t * t) * (c * (1.0 + 3.0 * 0.044715 * square))
    return pre * half, slope * tan_pre


def columns_to_rows(columns):
    lane = lax.broadcasted_iota(jnp.int32, (BLK, BLK), 1)
    packed = jnp.zeros((BLK, BLK), F32)
    for n, column in enumerate(columns):
        packed = jnp.where(lane == n, column, packed)
    return packed.T[0:8]


def rows_to_columns(rows):
    return jnp.concatenate([rows, jnp.zeros((BLK - 8, BLK), F32)], axis=0).T


def body(
    lat, probes, mod, gains, pattern, wqkv_hbm, wout_hbm, wup_hbm, wdn_hbm,
    lat_out, dens_out,
    wqkv, wout, wmlp, kv_first, kv_second, x, signs, proj, queries, hid, attn, acc, part, got, tot, stat, dens,
    w_sem, s_send, s_recv, x_send, x_recv, f_send, f_recv, r_send, r_recv, p_send, p_recv,
    d_send, d_recv, *ring_sems,
):
    ctx, tp, core = place()
    mine = feature_cols(tp)
    rows_sent = pl.ds(pl.multiple_of(core * HALF, HALF), 3 * HALF)
    full = float(D)
    shard = pl.ds(pl.multiple_of(ctx * SHARD, 64), SHARD)
    loads = [
        pltpu.make_async_copy(wup_hbm, wmlp.at[0, shard], w_sem.at[0]),
        pltpu.make_async_copy(wdn_hbm, wmlp.at[1, shard], w_sem.at[1]),
        pltpu.make_async_copy(wqkv_hbm.at[1], wqkv.at[:, 0:W], w_sem.at[2]),
        pltpu.make_async_copy(wqkv_hbm.at[2], wqkv.at[:, W : 2 * W], w_sem.at[3]),
        pltpu.make_async_copy(wqkv_hbm.at[0], wqkv.at[:, 2 * W : 3 * W], w_sem.at[4]),
        pltpu.make_async_copy(wout_hbm, wout, w_sem.at[5]),
    ]
    for load in loads:
        load.start()
    signs[...] = 2.0 * probes[...].astype(F32) - 1.0
    lat_out[...] = lat[...]
    right, left, across = ring_devices()
    greet([tp_at(i) for i in range(1, NTP)] + [right, left, across, sibling()])

    def block_rows(block):
        return pl.ds(pl.multiple_of(block * SHARD, 64), SHARD)

    weight_ring = Ring(
        lambda block: wmlp.at[core, block_rows(block)],
        lambda block: wmlp.at[core, block_rows(block)],
        lambda block: wmlp.at[1 - core, block_rows(block)],
        [sems.at[STEPS] for sems in ring_sems],
    )
    loads[0].wait()
    loads[1].wait()
    weight_ring.start()
    change = jnp.zeros((BLK, 1), F32)

    for step in range(STEPS):
        copies = []
        kv = (kv_first, kv_second)[step]
        rows, tangent = lat_out[...], signs[...]
        stat[tp] = columns_to_rows(
            [
                jnp.sum(rows, 1, keepdims=True),
                jnp.sum(rows * rows, 1, keepdims=True),
                jnp.sum(tangent, 1, keepdims=True),
                jnp.sum(rows * tangent, 1, keepdims=True),
            ]
        )
        for i in range(1, NTP):
            copy = remote(
                stat.at[tp], stat.at[tp], s_send.at[step, i], s_recv.at[step, i], tp_at(i)
            )
            copy.start()
            copies.append(copy)
        for i in range(1, NTP):
            there = stat.at[lax.rem(tp - i + NTP, NTP)]
            remote(there, there, s_send.at[step, i], s_recv.at[step, i], tp_at(i)).wait_recv()
        total = stat[0]
        for n in range(1, NTP):
            total = total + stat[n]
        total = rows_to_columns(total) * (1.0 / full)
        row_mean, row_sq, tan_mean, tan_sq = (total[:, n : n + 1] for n in range(4))
        row_var = row_sq - row_mean * row_mean
        tan_var = 2.0 * (tan_sq - row_mean * tan_mean)
        inv_std = lax.rsqrt(row_var + EPS)
        centred = rows - row_mean
        shift, gain = mod[3 * step : 3 * step + 1], 1.0 + mod[3 * step + 1 : 3 * step + 2]
        normed = (centred * inv_std * gain + shift).astype(BF16)
        tan_normed = (tangent - tan_mean) * inv_std - 0.5 * centred * (
            inv_std * inv_std * inv_std * tan_var
        )
        x[0:HALF, mine] = normed[0:HALF]
        x[HALF : 3 * HALF, mine] = (tan_normed * gain).astype(BF16)
        x[3 * HALF : ROWS, mine] = normed[HALF:BLK]
        for i in range(1, NTP):
            here = x.at[rows_sent, mine]
            copy = remote(here, here, x_send.at[step, i], x_recv.at[step, i], tp_at(i))
            copy.start()
            copies.append(copy)
        if step == 0:
            weight_ring.advance(2)
        for i in range(1, NTP):
            cols = feature_cols(lax.rem(tp - i + NTP, NTP))
            here = x.at[rows_sent, cols]
            remote(here, here, x_send.at[step, i], x_recv.at[step, i], tp_at(i)).wait_recv()
            piece = x.at[half_rows(core), cols]
            copy = remote(piece, piece, f_send.at[step, i], f_recv.at[step, i], sibling())
            copy.start()
            copies.append(copy)
            if step == 0 and i in (2, 4, 6):
                weight_ring.advance(1)
        for i in range(1, NTP):
            piece = x.at[half_rows(1 - core), feature_cols(lax.rem(tp - i + NTP, NTP))]
            remote(piece, piece, f_send.at[step, i], f_recv.at[step, i], sibling()).wait_recv()
        if step == 0:
            for load in loads[2:]:
                load.wait()

        def head_pair(column, gain_row, h):
            view = proj[:, column + h * HD : column + (h + 1) * HD]
            primal = jnp.concatenate([view[0:HALF], view[3 * HALF : ROWS]], axis=0)
            tan = view[HALF : 3 * HALF]
            gain_view = gains[gain_row : gain_row + 1, h * HD : (h + 1) * HD]
            inv = lax.rsqrt(jnp.mean(primal * primal, 1, keepdims=True) + EPS)
            tan_inv = -inv * inv * inv * jnp.mean(primal * tan, 1, keepdims=True)
            return (
                (primal * inv * gain_view).astype(BF16),
                ((tan * inv + primal * tan_inv) * gain_view).astype(BF16),
            )

        def project(start, stop):
            proj[:, start:stop] = jnp.dot(
                x[...], wqkv[:, start:stop], preferred_element_type=F32
            )

        for n in range(3):
            project(256 * n, 256 * (n + 1))
        if step == 0:
            weight_ring.advance(1)
        for h in range(HEADS):
            cols = slice(h * HD, (h + 1) * HD)
            key, tan_key = head_pair(0, 1, h)
            kv[ctx, 0, :, cols] = key
            kv[ctx, 1, :, cols] = tan_key
        kv[ctx, 2] = proj[HALF : 3 * HALF, W : 2 * W].astype(BF16)
        kv[ctx, 3, 0:HALF] = proj[0:HALF, W : 2 * W].astype(BF16)
        kv[ctx, 3, HALF:BLK] = proj[3 * HALF : ROWS, W : 2 * W].astype(BF16)
        kv_ring = Ring(
            lambda block, kv=kv: kv.at[block, pl.ds(core, 3)],
            lambda block, kv=kv: kv.at[block, pl.ds(core * 3, 1)],
            lambda block, kv=kv: kv.at[block, pl.ds((1 - core) * 3, 1)],
            [sems.at[step] for sems in ring_sems],
        )
        kv_ring.start()
        if step == 0:
            weight_ring.advance(2)
        project(768, 1152)
        for h in range(HEADS):
            query, tan_query = head_pair(768, 0, h)
            queries[0:BLK, h * HD : (h + 1) * HD] = query
            queries[BLK:ROWS, h * HD : (h + 1) * HD] = tan_query
        if step == 0:
            while weight_ring.todo:
                weight_ring.advance(2)
                kv_ring.advance(1)
            weight_ring.finish()
        else:
            kv_ring.advance(2)
        for n in range(3):
            cols = slice(256 * n, 256 * (n + 1))
            pre = jnp.dot(x[...], wmlp[0, :, cols], preferred_element_type=F32)
            primal = jnp.concatenate([pre[0:HALF], pre[3 * HALF : ROWS]], axis=0)
            hidden, tan_hidden = gelu_pair(primal, pre[HALF : 3 * HALF])
            hidden = hidden.astype(BF16)
            hid[0:HALF, cols] = hidden[0:HALF]
            hid[HALF : 3 * HALF, cols] = tan_hidden.astype(BF16)
            hid[3 * HALF : ROWS, cols] = hidden[HALF:BLK]
            kv_ring.advance(1)
        for n in range(4):
            cols = slice(768 * n, 768 * (n + 1))
            acc[:, cols] = lax.dot_general(
                hid[...],
                wmlp[1, cols, :],
                (((1,), (1,)), ((), ())),
                preferred_element_type=F32,
            )
            kv_ring.advance(2)
        kv_ring.finish()
        first = pattern[0, 0]
        listed = [pattern[0, j] for j in range(K_SEL)]
        penalty = [
            jnp.where(listed[j] == first, NEG_BIG, 0.0).astype(F32) if j else None
            for j in range(K_SEL)
        ]
        scale = 1.0 / math.sqrt(HD)
        contract = (((1,), (1,)), ((), ()))
        for h in range(HEADS):
            cols = slice(h * HD, (h + 1) * HD)
            pair = queries[:, cols]
            scores, tan_scores = [], []
            for j in range(K_SEL):
                key, tan_key = kv[listed[j], 0, :, cols], kv[listed[j], 1, :, cols]
                both = lax.dot_general(pair, key, contract, preferred_element_type=F32) * scale
                cross = lax.dot_general(
                    pair[0:BLK], tan_key, contract, preferred_element_type=F32
                )
                score = both[0:BLK]
                scores.append(score + penalty[j] if j else score)
                tan_scores.append(both[BLK:ROWS] + cross * scale)
            top = scores[0]
            for j in range(1, K_SEL):
                top = jnp.maximum(top, scores[j])
            top = jnp.max(top, 1, keepdims=True)
            out = jnp.zeros((ROWS, 2 * HD), F32)
            weight_sum, tan_sum = jnp.zeros((BLK, BLK), F32), jnp.zeros((BLK, BLK), F32)
            for j in range(K_SEL):
                weights = jnp.exp(scores[j] - top)
                weighted = weights * tan_scores[j]
                weight_sum, tan_sum = weight_sum + weights, tan_sum + weighted
                left_side = jnp.concatenate([weights, weighted], axis=0).astype(BF16)
                values = jnp.concatenate(
                    [kv[listed[j], 3, :, cols], kv[listed[j], 2, :, cols]], axis=1
                )
                out = out + jnp.dot(left_side, values, preferred_element_type=F32)
            inv = 1.0 / jnp.sum(weight_sum, 1, keepdims=True)
            ratio = jnp.sum(tan_sum, 1, keepdims=True) * inv
            output = out[0:BLK, 0:HD] * inv
            tan_output = (out[0:BLK, HD : 2 * HD] + out[BLK:ROWS, 0:HD]) * inv - ratio * output
            output = output.astype(BF16)
            attn[0:HALF, cols] = output[0:HALF]
            attn[HALF : 3 * HALF, cols] = tan_output.astype(BF16)
            attn[3 * HALF : ROWS, cols] = output[HALF:BLK]
        for copy in copies:
            copy.wait_send()
        copies = []
        for i in range(1, NTP + 1):
            cols = feature_cols(lax.rem(tp + i, NTP))
            part[i % NTP] = (
                acc[:, cols] + jnp.dot(attn[...], wout[:, cols], preferred_element_type=F32)
            ).astype(BF16)
            if i < NTP:
                copy = remote(
                    part.at[i, rows_sent],
                    got.at[i],
                    r_send.at[step, i],
                    r_recv.at[step, i],
                    tp_at(i),
                )
                copy.start()
                copies.append(copy)
        total = part[0, rows_sent].astype(F32)
        for i in range(1, NTP):
            remote(
                got.at[i], got.at[i], r_send.at[step, i], r_recv.at[step, i], tp_at(i)
            ).wait_recv()
            total = total + got[i].astype(F32)
        tot[rows_sent] = total
        piece, other = tot.at[half_rows(core)], tot.at[half_rows(1 - core)]
        copy = remote(piece, piece, p_send.at[step], p_recv.at[step], sibling())
        copy.start()
        copies.append(copy)
        gate = mod[3 * step + 2 : 3 * step + 3]
        change = change + jnp.sum(
            signs[...] * (gate * tot[HALF : 3 * HALF]), axis=1, keepdims=True
        )
        remote(other, other, p_send.at[step], p_recv.at[step], sibling()).wait_recv()
        lat_out[0:HALF] += (1.0 / STEPS) * (gate * tot[0:HALF])
        lat_out[HALF:BLK] += (1.0 / STEPS) * (gate * tot[3 * HALF : ROWS])
        for copy in copies:
            copy.wait_send()
        kv_ring.drain()
        if step == 0:
            weight_ring.drain()

    copies = []
    dens[tp] = columns_to_rows([change])
    for i in range(1, NTP):
        copy = remote(dens.at[tp], dens.at[tp], d_send.at[i], d_recv.at[i], tp_at(i))
        copy.start()
        copies.append(copy)
    for i in range(1, NTP):
        there = dens.at[lax.rem(tp - i + NTP, NTP)]
        remote(there, there, d_send.at[i], d_recv.at[i], tp_at(i)).wait_recv()
    total = dens[0]
    for n in range(1, NTP):
        total = total + dens[n]
    dens[NTP] = total
    copy = remote(dens.at[NTP], dens.at[NTP + 1], d_send.at[0], d_recv.at[0], sibling())
    copy.start()
    remote(dens.at[NTP + 1], dens.at[NTP + 1], d_send.at[0], d_recv.at[0], sibling()).wait_recv()
    copies.append(copy)
    dens_out[...] = (dens[NTP] + dens[NTP + 1]) * (-1.0 / (STEPS * 2 * math.sqrt(full)))
    for copy in copies:
        copy.wait_send()


def local(latent, probes, modulation, pattern, w_qkv, w_out, w_up, w_down, q_gain, k_gain):
    start = lax.axis_index("tp") * W
    mod = lax.dynamic_slice_in_dim(modulation.reshape(3 * STEPS, D), start, W, 1)
    gains = jnp.stack([q_gain, k_gain])
    vmem, anywhere = pl.BlockSpec(memory_space=pltpu.VMEM), pl.BlockSpec(memory_space=pl.ANY)
    dma = pltpu.SemaphoreType.DMA
    latent_out, density = pl.pallas_call(
        body,
        out_shape=(
            jax.ShapeDtypeStruct((BLK, W), F32),
            jax.ShapeDtypeStruct((8, BLK), F32),
        ),
        in_specs=[vmem] * 4 + [pl.BlockSpec(memory_space=pltpu.SMEM)] + [anywhere] * 4,
        out_specs=(vmem, vmem),
        scratch_shapes=[
            pltpu.VMEM((D, 3 * W), BF16),
            pltpu.VMEM((W, D), BF16),
            pltpu.VMEM((2, D, UNITS), BF16),
            pltpu.VMEM((NCTX, 4, BLK, W), BF16),
            pltpu.VMEM((NCTX, 4, BLK, W), BF16),
            pltpu.VMEM((ROWS, D), BF16),
            pltpu.VMEM((BLK, W), F32),
            pltpu.VMEM((ROWS, 3 * W), F32),
            pltpu.VMEM((ROWS, W), BF16),
            pltpu.VMEM((ROWS, UNITS), BF16),
            pltpu.VMEM((ROWS, W), BF16),
            pltpu.VMEM((ROWS, D), F32),
            pltpu.VMEM((NTP, ROWS, W), BF16),
            pltpu.VMEM((NTP, 3 * HALF, W), BF16),
            pltpu.VMEM((ROWS, W), F32),
            pltpu.VMEM((NTP, 8, BLK), F32),
            pltpu.VMEM((NTP + 2, 8, BLK), F32),
            dma((6,)),
        ]
        + [dma((STEPS, NTP)) for _ in range(8)]
        + [dma((STEPS,)) for _ in range(2)]
        + [dma((NTP,)) for _ in range(2)]
        + [dma((STEPS + 1, 15)) for _ in range(4)],
        compiler_params=pltpu.CompilerParams(
            collective_id=1, has_side_effects=True, vmem_limit_bytes=60 * 1024 * 1024
        ),
        name="euler_steps",
    )(
        latent,
        probes[0],
        mod,
        gains,
        pattern,
        w_qkv.transpose(1, 0, 2),
        w_out,
        w_up,
        w_down.T,
    )
    return latent_out, density[0]


def solution(mesh):
    return jax.shard_map(
        local,
        mesh=mesh,
        in_specs=(
            P("ctx", "tp"),
            P("probe", "ctx", "tp"),
            P(),
            P("ctx", None),
            P(None, None, "tp"),
            P("tp", None),
            P("ctx", "tp"),
            P("tp", "ctx"),
            P("tp"),
            P("tp"),
        ),
        out_specs=(P("ctx", "tp"), P("ctx")),
        check_vma=False,
    )
```

time: 1220 us -> 244 us (0.20)
  waiting for transfers between devices: 892 us -> 0 us
  Pallas kernels: 0 us -> 236 us
  blocking collectives: 160 us -> 0 us
  local copies, waits for them, and re-layouts: 76.3 us -> 5.73 us
  matrix products: 42.8 us -> 0 us
  other arithmetic: 27.4 us -> 0.6 us
  between operations: 14.8 us -> 0.66 us
    all_gather x10 -> x0, waiting for transfers between devices: 802 us -> none  [the longest x2 159 us: local(): lax.all_gather(dv_rows, 'ctx', axis=0, tiled=True)]
    pallas_call x0 -> x1, Pallas kernels: none -> 236 us  [local(): pl.pallas_call(body, out_shape=(jax.ShapeDtypeStruct((BLK, W), F32), jax....]
    all_gather x4 -> x0, blocking collectives: 98.3 us -> none  [the longest x2 49.3 us: norm_features(): lax.all_gather(tangent_act, 'tp', axis=1, tiled=True)]
    unnamed x14 -> x0, waiting for transfers between devices: 90.1 us -> none
    psum x3 -> x0, blocking collectives: 61.8 us -> none  [the longest x2 31.4 us: norm_features(): totals = lax.psum(row_sums, 'tp')]
    dot_general x20 -> x0, matrix products: 42.8 us -> none  [the longest x2 12.6 us: local(): jnp.einsum('rd,dcf->crf', stacked, w_qkv, preferred_element_type=jnp.floa...]
    gather x8 -> x0, local copies, waits for them, and re-layouts: 22.4 us -> none  [select_blocks(): jnp.take(blocked, chosen, axis=0).reshape(K_SEL * BLK, heads_local, HD)]
    reshape x8 -> x1, local copies, waits for them, and re-layouts: 17.1 us -> 0.04 us  [local(): modulation.reshape(3 * STEPS, D)]
  transfers between devices with their start and end apart: 12 -> 0, of which waited for: 12 -> 0; matrix products, arithmetic and copies ran while one was open for 7% -> 0% of each run, Pallas kernels for 0% -> 0%
where the time goes in v2:
time: 244 us; the launch traced here: 243 us
  Pallas kernels  236 us (97%)
  local copies, waits for them, and re-layouts  5.73 us (2%)
    pallas_call x1, Pallas kernels, local(): pl.pallas_call(body, out_shape=(jax.ShapeDtypeStruct((BLK, W), F32), jax....  236 us

profile of v2, /device:TPU:1, one launch (start us, length us, event | category | flops | bytes accessed | tf_op | source)
XLA Modules:
  0.0 243.4 jit_solution(12263411905949748387)
XLA Ops:
  0.6 0.7 stack.9
  1.3 0.7 stack.10
  2.0 0.6 pad_maximum_fusion.gains
  2.6 0.9 copy.13
  3.6 0.6 constant_dynamic-slice_fusion.mod
  4.2 236.4 %euler_steps.1 = (f32[128,384]{1,0:T(8,128)}, f32[8,128]{1,0:T(8,128)}) custom-call(f32[128,384]{1,0:T(8,128)} %lat.1, s32[128,384]{1,0:T(8,128)} %bitcast.7, f32[6,384]{1,0:T(8,128)} %constant_dynamic-slice_fusion.mod, f32[2,384]{1,0:T(2,128)} %pad_maximum_fusion.gains, s32[1,8]{1,0:T(1,128)} %pattern.1, bf16[3,3072,384]{2,1,0:T(8,128)(2,1)} %bitcast.5, ...), custom_call_target="tpu_custom_call" | custom-call | tf_op jit(solution)/shard_map/euler_steps/pallas_call | solution.py:457
  240.6 1.2 slice_bitcast_fusion
  241.8 1.6 copy.15
  (1 shorter events, 0.0 us)

commit v3 on v2

--- a/solution.py
+++ b/solution.py
@@ -80,6 +80,10 @@
     return pl.ds(pl.multiple_of(owner * W, 128), W)
 
 
+def head_cols(owner):
+    return pl.ds(pl.multiple_of(owner * HD, 128), HD)
+
+
 def half_rows(core):
     return pl.ds(pl.multiple_of(core * 3 * HALF, HALF), HALF)
 
@@ -88,58 +92,126 @@
     def __init__(self, own, passed, given, sems):
         self.own, self.passed, self.given = own, passed, given
         self.send, self.recv, self.f_send, self.f_recv = sems
-        ctx, _, _ = place()
+        ctx, _, core = place()
         z, h = lax.rem(ctx, NZ), lax.div(ctx, NZ)
         self.ctx = ctx
-        self.right, self.left, self.across = ring_devices()
+        right, left, across = ring_devices()
+        turn = 1 - 2 * core
+        ahead = ctx_at(h * NZ + lax.rem(z + turn + NZ, NZ))
+        behind = ctx_at(h * NZ + lax.rem(z - turn + NZ, NZ))
+        self.right, self.left, self.across, self.ahead, self.behind = right, left, across, ahead, behind
         self.copies, self.taken = [], []
 
         def at(row, step):
             return row * NZ + lax.rem(z + step + NZ, NZ)
 
-        self.beside = at(1 - h, 0)
-        self.todo = [(self.beside, 0, ((5, self.right), (11, self.left)))]
+        self.todo = [
+            (at(1 - h, 0), 0, 0, ((5, right), (11, left))),
+            (at(1 - h, 0), 1, 22, ()),
+        ]
         for s in range(1, 5):
             for row, step, base, reach, device in (
-                (h, -s, 0, 4, self.right),
-                (h, s, 7, 3, self.left),
-                (1 - h, -s, 4, 3, self.right),
-                (1 - h, s, 10, 4, self.left),
+                (h, -s, 0, 4, right),
+                (h, s, 7, 3, left),
             ):
                 if s <= reach:
                     onward = ((base + s + 1, device),) if s < reach else ()
-                    self.todo.append((at(row, step), base + s, onward))
-
-    def push(self, block, n, device):
-        copy = remote(self.own(block), self.own(block), self.send.at[n], self.recv.at[n], device)
+                    self.todo.append((at(row, step), 0, base + s, onward))
+            for step, base, y_base, reach, device in (
+                (-s * turn, 14, 22, 4, ahead),
+                (s * turn, 18, 26, 3, behind),
+            ):
+                if s <= reach:
+                    onward = ((base + s + 1, device),) if s < reach else ()
+                    onward = onward + ((y_base + s, across),)
+                    self.todo.append((at(h, step), 1, base + s, onward))
+            for row, step, base, reach, device in (
+                (1 - h, -s, 4, 3, right),
+                (1 - h, s, 10, 4, left),
+            ):
+                if s <= reach:
+                    onward = ((base + s + 1, device),) if s < reach else ()
+                    self.todo.append((at(row, step), 0, base + s, onward))
+            self.todo.append((at(1 - h, -s * turn), 1, 22 + s, ()))
+            if s <= 3:
+                self.todo.append((at(1 - h, s * turn), 1, 26 + s, ()))
+
+    def push(self, block, part, n, device):
+        piece = self.own(block, part)
+        copy = remote(piece, piece, self.send.at[n], self.recv.at[n], device)
         copy.start()
         self.copies.append(copy)
 
     def start(self):
-        self.push(self.ctx, 0, self.across)
-        self.push(self.ctx, 1, self.right)
-        self.push(self.ctx, 8, self.left)
+        self.push(self.ctx, 0, 0, self.across)
+        self.push(self.ctx, 0, 1, self.right)
+        self.push(self.ctx, 0, 8, self.left)
+        self.push(self.ctx, 1, 15, self.ahead)
+        self.push(self.ctx, 1, 19, self.behind)
+        self.push(self.ctx, 1, 22, self.across)
 
     def advance(self, count=1):
         for _ in range(count):
             if not self.todo:
                 return
-            block, n, onward = self.todo.pop(0)
-            mine = self.own(block)
+            block, part, n, onward = self.todo.pop(0)
+            mine = self.own(block, part)
             remote(mine, mine, self.send.at[n], self.recv.at[n], self.across).wait_recv()
             for later, device in onward:
-                self.push(block, later, device)
-            piece = self.passed(block)
+                self.push(block, part, later, device)
+            piece = self.passed(block, part)
             copy = remote(piece, piece, self.f_send.at[n], self.f_recv.at[n], sibling())
             copy.start()
             self.copies.append(copy)
-            self.taken.append((block, n))
+            self.taken.append((block, part, n))
 
     def finish(self):
         self.advance(len(self.todo))
-        for block, n in self.taken:
-            piece = self.given(block)
+        for block, part, n in self.taken:
+            piece = self.given(block, part)
             remote(piece, piece, self.f_send.at[n], self.f_recv.at[n], sibling()).wait_recv()
+
+    def drain(self):
+        for copy in self.copies:
+            copy.wait_send()
+
+
+class Share:
+    def __init__(self, piece, passed, given, sems, source=None):
+        self.piece, self.passed, self.given = piece, passed, given
+        self.send, self.recv, self.f_send, self.f_recv = sems
+        self.tp = lax.axis_index("tp")
+        self.source = source or (lambda i: piece(self.tp))
+        self.copies = []
+        self.next = 1
+
+    def owner(self, i):
+        return lax.rem(self.tp - i + NTP, NTP)
+
+    def push(self):
+        for i in range(1, NTP):
+            copy = remote(
+                self.source(i), self.piece(self.tp), self.send.at[i], self.recv.at[i], tp_at(i)
+            )
+            copy.start()
+            self.copies.append(copy)
+
+    def collect(self, count=NTP):
+        while self.next < NTP and count:
+            i, owner = self.next, self.owner(self.next)
+            here = self.piece(owner)
+            remote(here, here, self.send.at[i], self.recv.at[i], tp_at(i)).wait_recv()
+            part = self.passed(owner)
+            copy = remote(part, part, self.f_send.at[i], self.f_recv.at[i], sibling())
+            copy.start()
+            self.copies.append(copy)
+            self.next, count = self.next + 1, count - 1
+
+    def finish(self):
+        self.collect()
+        for i in range(1, NTP):
+            part = self.given(self.owner(i))
+            remote(part, part, self.f_send.at[i], self.f_recv.at[i], sibling()).wait_recv()
 
     def drain(self):
         for copy in self.copies:
@@ -170,13 +242,17 @@
 def body(
     lat, probes, mod, gains, pattern, wqkv_hbm, wout_hbm, wup_hbm, wdn_hbm,
     lat_out, dens_out,
-    wqkv, wout, wmlp, kv_first, kv_second, x, signs, proj, queries, hid, attn, acc, part, got, tot, stat, dens,
-    w_sem, s_send, s_recv, x_send, x_recv, f_send, f_recv, r_send, r_recv, p_send, p_recv,
-    d_send, d_recv, *ring_sems,
+    kv_0, kv_1, kv_2, kv_3, kv_4, kv_5,
+    wqkv, wo, wmlp, x, xa_0, xa_1, xa_2, signs, proj, queries, hid, acc, part, got, tot, stat, dens,
+    w_sem, s_send, s_recv, r_send, r_recv, p_send, p_recv, d_send, d_recv,
+    *many_sems,
 ):
+    ring_sems, share_sems = many_sems[:4], many_sems[4:]
     ctx, tp, core = place()
     mine = feature_cols(tp)
     rows_sent = pl.ds(pl.multiple_of(core * HALF, HALF), 3 * HALF)
+    my_half = pl.ds(pl.multiple_of(core * HALF, HALF), HALF)
+    other_half = pl.ds(pl.multiple_of((1 - core) * HALF, HALF), HALF)
     full = float(D)
     shard = pl.ds(pl.multiple_of(ctx * SHARD, 64), SHARD)
     loads = [
@@ -185,7 +261,7 @@
         pltpu.make_async_copy(wqkv_hbm.at[1], wqkv.at[:, 0:W], w_sem.at[2]),
         pltpu.make_async_copy(wqkv_hbm.at[2], wqkv.at[:, W : 2 * W], w_sem.at[3]),
         pltpu.make_async_copy(wqkv_hbm.at[0], wqkv.at[:, 2 * W : 3 * W], w_sem.at[4]),
-        pltpu.make_async_copy(wout_hbm, wout, w_sem.at[5]),
+        pltpu.make_async_copy(wout_hbm.at[:, :, mine], wo.at[:, tp], w_sem.at[5]),
     ]
     for load in loads:
         load.start()
@@ -194,14 +270,21 @@
     right, left, across = ring_devices()
     greet([tp_at(i) for i in range(1, NTP)] + [right, left, across, sibling()])
 
-    def block_rows(block):
-        return pl.ds(pl.multiple_of(block * SHARD, 64), SHARD)
+    def block_rows(block, part):
+        return pl.ds(pl.multiple_of(block * SHARD + part * (SHARD // 2), 32), SHARD // 2)
 
     weight_ring = Ring(
-        lambda block: wmlp.at[core, block_rows(block)],
-        lambda block: wmlp.at[core, block_rows(block)],
-        lambda block: wmlp.at[1 - core, block_rows(block)],
-        [sems.at[STEPS] for sems in ring_sems],
+        lambda block, part: wmlp.at[core, block_rows(block, part)],
+        lambda block, part: wmlp.at[core, block_rows(block, part)],
+        lambda block, part: wmlp.at[1 - core, block_rows(block, part)],
+        [sems.at[STEPS * HEADS] for sems in ring_sems],
+    )
+    wout_share = Share(
+        lambda owner: wo.at[:, owner, my_half],
+        lambda owner: wo.at[:, owner, my_half],
+        lambda owner: wo.at[:, owner, other_half],
+        [sems.at[STEPS * (HEADS + 1)] for sems in share_sems],
+        lambda i: wout_hbm.at[:, my_half, feature_cols(lax.rem(tp + i, NTP))],
     )
     loads[0].wait()
     loads[1].wait()
@@ -210,7 +293,8 @@
 
     for step in range(STEPS):
         copies = []
-        kv = (kv_first, kv_second)[step]
+        kvs = (kv_0, kv_1, kv_2, kv_3, kv_4, kv_5)[HEADS * step : HEADS * (step + 1)]
+        xas = (xa_0, xa_1, xa_2)
         rows, tangent = lat_out[...], signs[...]
         stat[tp] = columns_to_rows(
             [
@@ -246,26 +330,19 @@
         x[0:HALF, mine] = normed[0:HALF]
         x[HALF : 3 * HALF, mine] = (tan_normed * gain).astype(BF16)
         x[3 * HALF : ROWS, mine] = normed[HALF:BLK]
-        for i in range(1, NTP):
-            here = x.at[rows_sent, mine]
-            copy = remote(here, here, x_send.at[step, i], x_recv.at[step, i], tp_at(i))
-            copy.start()
-            copies.append(copy)
+        x_share = Share(
+            lambda owner: x.at[rows_sent, feature_cols(owner)],
+            lambda owner: x.at[half_rows(core), feature_cols(owner)],
+            lambda owner: x.at[half_rows(1 - core), feature_cols(owner)],
+            [sems.at[step] for sems in share_sems],
+        )
+        x_share.push()
         if step == 0:
             weight_ring.advance(2)
-        for i in range(1, NTP):
-            cols = feature_cols(lax.rem(tp - i + NTP, NTP))
-            here = x.at[rows_sent, cols]
-            remote(here, here, x_send.at[step, i], x_recv.at[step, i], tp_at(i)).wait_recv()
-            piece = x.at[half_rows(core), cols]
-            copy = remote(piece, piece, f_send.at[step, i], f_recv.at[step, i], sibling())
-            copy.start()
-            copies.append(copy)
-            if step == 0 and i in (2, 4, 6):
-                weight_ring.advance(1)
-        for i in range(1, NTP):
-            piece = x.at[half_rows(1 - core), feature_cols(lax.rem(tp - i + NTP, NTP))]
-            remote(piece, piece, f_send.at[step, i], f_recv.at[step, i], sibling()).wait_recv()
+            for _ in range(3):
+                x_share.collect(2)
+                weight_ring.advance(2)
+        x_share.finish()
         if step == 0:
             for load in loads[2:]:
                 load.wait()
@@ -287,27 +364,46 @@
                 x[...], wqkv[:, start:stop], preferred_element_type=F32
             )
 
+        def own_block(h):
+            kv = kvs[h]
+            key, tan_key = head_pair(0, 1, h)
+            cols = slice(W + h * HD, W + (h + 1) * HD)
+            kv[ctx, 0] = key
+            kv[ctx, 1] = tan_key
+            kv[ctx, 2] = proj[HALF : 3 * HALF, cols].astype(BF16)
+            kv[ctx, 3, 0:HALF] = proj[0:HALF, cols].astype(BF16)
+            kv[ctx, 3, HALF:BLK] = proj[3 * HALF : ROWS, cols].astype(BF16)
+
+        def part_rows(part):
+            return slice(part * HALF, (part + 1) * HALF)
+
+        rings = [
+            Ring(
+                lambda block, part, kv=kv: kv.at[block, pl.ds(core, 3), part_rows(part)],
+                lambda block, part, kv=kv: kv.at[block, pl.ds(core * 3, 1), part_rows(part)],
+                lambda block, part, kv=kv: kv.at[block, pl.ds((1 - core) * 3, 1), part_rows(part)],
+                [sems.at[step * HEADS + h] for sems in ring_sems],
+            )
+            for h, kv in enumerate(kvs)
+        ]
+        shares = [
+            Share(
+                lambda owner, xa=xa: xa.at[rows_sent, head_cols(owner)],
+                lambda owner, xa=xa: xa.at[half_rows(core), head_cols(owner)],
+                lambda owner, xa=xa: xa.at[half_rows(1 - core), head_cols(owner)],
+                [sems.at[STEPS + step * HEADS + h] for sems in share_sems],
+            )
+            for h, xa in enumerate(xas)
+        ]
         for n in range(3):
             project(256 * n, 256 * (n + 1))
+        own_block(0)
+        rings[0].start()
         if step == 0:
-            weight_ring.advance(1)
-        for h in range(HEADS):
-            cols = slice(h * HD, (h + 1) * HD)
-            key, tan_key = head_pair(0, 1, h)
-            kv[ctx, 0, :, cols] = key
-            kv[ctx, 1, :, cols] = tan_key
-        kv[ctx, 2] = proj[HALF : 3 * HALF, W : 2 * W].astype(BF16)
-        kv[ctx, 3, 0:HALF] = proj[0:HALF, W : 2 * W].astype(BF16)
-        kv[ctx, 3, HALF:BLK] = proj[3 * HALF : ROWS, W : 2 * W].astype(BF16)
-        kv_ring = Ring(
-            lambda block, kv=kv: kv.at[block, pl.ds(core, 3)],
-            lambda block, kv=kv: kv.at[block, pl.ds(core * 3, 1)],
-            lambda block, kv=kv: kv.at[block, pl.ds((1 - core) * 3, 1)],
-            [sems.at[step] for sems in ring_sems],
-        )
-        kv_ring.start()
-        if step == 0:
-            weight_ring.advance(2)
+            weight_ring.advance(4)
+            wout_share.push()
+        own_block(1)
+        own_block(2)
         project(768, 1152)
         for h in range(HEADS):
             query, tan_query = head_pair(768, 0, h)
@@ -316,11 +412,21 @@
         if step == 0:
             while weight_ring.todo:
                 weight_ring.advance(2)
-                kv_ring.advance(1)
+                rings[0].advance(1)
             weight_ring.finish()
-        else:
-            kv_ring.advance(2)
-        for n in range(3):
+
+        spread = 15
+        agenda = []
+        for h in range(HEADS):
+            size = 2 + 28
+            for k in range(size - len(rings[h].todo), size):
+                agenda.append((k + spread * h, 1, h, "advance"))
+            if h:
+                agenda.append((spread * h - 6, 0, h, "start"))
+            agenda.append((size + spread * h, 2, h, "attend"))
+        agenda.sort()
+
+        def up(n):
             cols = slice(256 * n, 256 * (n + 1))
             pre = jnp.dot(x[...], wmlp[0, :, cols], preferred_element_type=F32)
             primal = jnp.concatenate([pre[0:HALF], pre[3 * HALF : ROWS]], axis=0)
@@ -329,17 +435,36 @@
             hid[0:HALF, cols] = hidden[0:HALF]
             hid[HALF : 3 * HALF, cols] = tan_hidden.astype(BF16)
             hid[3 * HALF : ROWS, cols] = hidden[HALF:BLK]
-            kv_ring.advance(1)
-        for n in range(4):
-            cols = slice(768 * n, 768 * (n + 1))
-            acc[:, cols] = lax.dot_general(
-                hid[...],
-                wmlp[1, cols, :],
-                (((1,), (1,)), ((), ())),
-                preferred_element_type=F32,
-            )
-            kv_ring.advance(2)
-        kv_ring.finish()
+
+        def down(i):
+            units = feature_cols(lax.rem(tp + i, NTP))
+            part[i % NTP] = lax.dot_general(
+                hid[...], wmlp[1, units, :], (((1,), (1,)), ((), ())), preferred_element_type=F32
+            ).astype(BF16)
+            if i < NTP:
+                copy = remote(
+                    part.at[i, rows_sent],
+                    got.at[i],
+                    r_send.at[step, i],
+                    r_recv.at[step, i],
+                    tp_at(i),
+                )
+                copy.start()
+                copies.append(copy)
+
+        def collect_parts():
+            total = part[0, rows_sent].astype(F32)
+            for i in range(1, NTP):
+                remote(
+                    got.at[i], got.at[i], r_send.at[step, i], r_recv.at[step, i], tp_at(i)
+                ).wait_recv()
+                total = total + got[i].astype(F32)
+            tot[rows_sent] = total
+            piece = tot.at[half_rows(core)]
+            copy = remote(piece, piece, p_send.at[step], p_recv.at[step], sibling())
+            copy.start()
+            copies.append(copy)
+
         first = pattern[0, 0]
         listed = [pattern[0, j] for j in range(K_SEL)]
         penalty = [
@@ -348,12 +473,13 @@
         ]
         scale = 1.0 / math.sqrt(HD)
         contract = (((1,), (1,)), ((), ()))
-        for h in range(HEADS):
-            cols = slice(h * HD, (h + 1) * HD)
-            pair = queries[:, cols]
+
+        def attend(h):
+            kv, xa = kvs[h], xas[h]
+            pair = queries[:, h * HD : (h + 1) * HD]
             scores, tan_scores = [], []
             for j in range(K_SEL):
-                key, tan_key = kv[listed[j], 0, :, cols], kv[listed[j], 1, :, cols]
+                key, tan_key = kv[listed[j], 0], kv[listed[j], 1]
                 both = lax.dot_general(pair, key, contract, preferred_element_type=F32) * scale
                 cross = lax.dot_general(
                     pair[0:BLK], tan_key, contract, preferred_element_type=F32
@@ -372,59 +498,63 @@
                 weighted = weights * tan_scores[j]
                 weight_sum, tan_sum = weight_sum + weights, tan_sum + weighted
                 left_side = jnp.concatenate([weights, weighted], axis=0).astype(BF16)
-                values = jnp.concatenate(
-                    [kv[listed[j], 3, :, cols], kv[listed[j], 2, :, cols]], axis=1
-                )
+                values = jnp.concatenate([kv[listed[j], 3], kv[listed[j], 2]], axis=1)
                 out = out + jnp.dot(left_side, values, preferred_element_type=F32)
             inv = 1.0 / jnp.sum(weight_sum, 1, keepdims=True)
             ratio = jnp.sum(tan_sum, 1, keepdims=True) * inv
             output = out[0:BLK, 0:HD] * inv
             tan_output = (out[0:BLK, HD : 2 * HD] + out[BLK:ROWS, 0:HD]) * inv - ratio * output
             output = output.astype(BF16)
-            attn[0:HALF, cols] = output[0:HALF]
-            attn[HALF : 3 * HALF, cols] = tan_output.astype(BF16)
-            attn[3 * HALF : ROWS, cols] = output[HALF:BLK]
+            cols = head_cols(tp)
+            xa[0:HALF, cols] = output[0:HALF]
+            xa[HALF : 3 * HALF, cols] = tan_output.astype(BF16)
+            xa[3 * HALF : ROWS, cols] = output[HALF:BLK]
+            shares[h].push()
+
+        def out_project(h):
+            more = jnp.dot(
+                xas[h][...], wo[h].reshape(NTP * HD, W), preferred_element_type=F32
+            )
+            acc[...] = more if h == 0 else acc[...] + more
+
+        tasks = [partial(up, n) for n in range(3)] + [partial(down, i) for i in range(1, NTP + 1)]
+        done = 0
+        for _, _, h, what in agenda:
+            if what == "start":
+                rings[h].start()
+            elif what == "advance":
+                rings[h].advance(1)
+                done += 1
+                if tasks and done % 2 == 0:
+                    tasks.pop(0)()
+            else:
+                rings[h].finish()
+                while h == 0 and tasks:
+                    tasks.pop(0)()
+                attend(h)
+                if h == 0 and step == 0:
+                    wout_share.finish()
+                if h == 1:
+                    shares[0].finish()
+                    out_project(0)
+                    collect_parts()
+        shares[1].finish()
+        out_project(1)
+        other = tot.at[half_rows(1 - core)]
+        remote(other, other, p_send.at[step], p_recv.at[step], sibling()).wait_recv()
+        shares[2].finish()
+        out_project(2)
+        branch = acc[...] + tot[...]
+        gate = mod[3 * step + 2 : 3 * step + 3]
+        change = change + jnp.sum(
+            signs[...] * (gate * branch[HALF : 3 * HALF]), axis=1, keepdims=True
+        )
+        lat_out[0:HALF] += (1.0 / STEPS) * (gate * branch[0:HALF])
+        lat_out[HALF:BLK] += (1.0 / STEPS) * (gate * branch[3 * HALF : ROWS])
         for copy in copies:
             copy.wait_send()
-        copies = []
-        for i in range(1, NTP + 1):
-            cols = feature_cols(lax.rem(tp + i, NTP))
-            part[i % NTP] = (
-                acc[:, cols] + jnp.dot(attn[...], wout[:, cols], preferred_element_type=F32)
-            ).astype(BF16)
-            if i < NTP:
-                copy = remote(
-                    part.at[i, rows_sent],
-                    got.at[i],
-                    r_send.at[step, i],
-                    r_recv.at[step, i],
-                    tp_at(i),
-                )
-                copy.start()
-                copies.append(copy)
-        total = part[0, rows_sent].astype(F32)
-        for i in range(1, NTP):
-            remote(
-                got.at[i], got.at[i], r_send.at[step, i], r_recv.at[step, i], tp_at(i)
-            ).wait_recv()
-            total = total + got[i].astype(F32)
-        tot[rows_sent] = total
-        piece, other = tot.at[half_rows(core)], tot.at[half_rows(1 - core)]
-        copy = remote(piece, piece, p_send.at[step], p_recv.at[step], sibling())
-        copy.start()
-        copies.append(copy)
-        gate = mod[3 * step + 2 : 3 * step + 3]
-        change = change + jnp.sum(
-            signs[...] * (gate * tot[HALF : 3 * HALF]), axis=1, keepdims=True
-        )
-        remote(other, other, p_send.at[step], p_recv.at[step], sibling()).wait_recv()
-        lat_out[0:HALF] += (1.0 / STEPS) * (gate * tot[0:HALF])
-        lat_out[HALF:BLK] += (1.0 / STEPS) * (gate * tot[3 * HALF : ROWS])
-        for copy in copies:
-            copy.wait_send()
-        kv_ring.drain()
-        if step == 0:
-            weight_ring.drain()
+        for part_of in rings + shares + [x_share] + ([weight_ring, wout_share] if step == 0 else []):
+            part_of.drain()
 
     copies = []
     dens[tp] = columns_to_rows([change])
@@ -462,19 +592,20 @@
         ),
         in_specs=[vmem] * 4 + [pl.BlockSpec(memory_space=pltpu.SMEM)] + [anywhere] * 4,
         out_specs=(vmem, vmem),
-        scratch_shapes=[
+        scratch_shapes=[pltpu.VMEM((NCTX, 4, BLK, HD), BF16) for _ in range(STEPS * HEADS)]
+        + [
             pltpu.VMEM((D, 3 * W), BF16),
-            pltpu.VMEM((W, D), BF16),
+            pltpu.VMEM((HEADS, NTP, HD, W), BF16),
             pltpu.VMEM((2, D, UNITS), BF16),
-            pltpu.VMEM((NCTX, 4, BLK, W), BF16),
-            pltpu.VMEM((NCTX, 4, BLK, W), BF16),
             pltpu.VMEM((ROWS, D), BF16),
+            pltpu.VMEM((ROWS, NTP * HD), BF16),
+            pltpu.VMEM((ROWS, NTP * HD), BF16),
+            pltpu.VMEM((ROWS, NTP * HD), BF16),
             pltpu.VMEM((BLK, W), F32),
             pltpu.VMEM((ROWS, 3 * W), F32),
             pltpu.VMEM((ROWS, W), BF16),
             pltpu.VMEM((ROWS, UNITS), BF16),
-            pltpu.VMEM((ROWS, W), BF16),
-            pltpu.VMEM((ROWS, D), F32),
+            pltpu.VMEM((ROWS, W), F32),
             pltpu.VMEM((NTP, ROWS, W), BF16),
             pltpu.VMEM((NTP, 3 * HALF, W), BF16),
             pltpu.VMEM((ROWS, W), F32),
@@ -482,10 +613,11 @@
             pltpu.VMEM((NTP + 2, 8, BLK), F32),
             dma((6,)),
         ]
-        + [dma((STEPS, NTP)) for _ in range(8)]
+        + [dma((STEPS, NTP)) for _ in range(4)]
         + [dma((STEPS,)) for _ in range(2)]
         + [dma((NTP,)) for _ in range(2)]
-        + [dma((STEPS + 1, 15)) for _ in range(4)],
+        + [dma((STEPS * HEADS + 1, 30)) for _ in range(4)]
+        + [dma((STEPS * (HEADS + 1) + 1, NTP)) for _ in range(4)],
         compiler_params=pltpu.CompilerParams(
             collective_id=1, has_side_effects=True, vmem_limit_bytes=60 * 1024 * 1024
         ),
@@ -497,7 +629,7 @@
         gains,
         pattern,
         w_qkv.transpose(1, 0, 2),
-        w_out,
+        w_out.reshape(HEADS, HD, D),
         w_up,
         w_down.T,
     )

time: 244 us -> 277 us (1.14)
  Pallas kernels: 236 us -> 270 us
    pallas_call x1, Pallas kernels: 236 us -> 270 us  [local(): pl.pallas_call(body, out_shape=(jax.ShapeDtypeStruct((BLK, W), F32), jax....]
where the time goes in v3:
time: 277 us
  Pallas kernels  270 us (97%)
  local copies, waits for them, and re-layouts  5.73 us (2%)
    pallas_call x1, Pallas kernels, local(): pl.pallas_call(body, out_shape=(jax.ShapeDtypeStruct((BLK, W), F32), jax....  270 us

profile of v3, /device:TPU:1, one launch (start us, length us, event | category | flops | bytes accessed | tf_op | source)
XLA Modules:
  0.0 276.9 jit_solution(895639029339987040)
XLA Ops:
  0.6 0.7 stack.9
  1.3 0.7 stack.10
  2.0 0.6 pad_maximum_fusion.gains
  2.6 0.9 copy.13
  3.6 0.6 constant_dynamic-slice_fusion.mod
  4.2 269.9 %euler_steps.1 = (f32[128,384]{1,0:T(8,128)}, f32[8,128]{1,0:T(8,128)}) custom-call(f32[128,384]{1,0:T(8,128)} %lat.1, s32[128,384]{1,0:T(8,128)} %bitcast.9, f32[6,384]{1,0:T(8,128)} %constant_dynamic-slice_fusion.mod, f32[2,384]{1,0:T(2,128)} %pad_maximum_fusion.gains, s32[1,8]{1,0:T(1,128)} %pattern.1, bf16[3,3072,384]{2,1,0:T(8,128)(2,1)} %bitcast.6, ...), custom_call_target="tpu_custom_call" | custom-call | tf_op jit(solution)/shard_map/euler_steps/pallas_call | solution.py:587
  274.1 1.2 slice_bitcast_fusion
  275.3 1.6 copy.15
  (1 shorter events, 0.0 us)

commit v4 on v3

--- a/solution.py
+++ b/solution.py
@@ -18,6 +18,8 @@
 W = 384
 D = 3072
 HEADS = 3
+GROUPS = ((0, 1), (2,))
+NG = len(GROUPS)
 UNITS = 768
 SHARD = 192
 HALF = 64
@@ -37,6 +39,11 @@
 def tp_at(offset):
     ctx, tp, core = place()
     return (ctx, lax.rem(tp + offset + NTP, NTP), core)
+
+
+def tp_of(x, y):
+    ctx, _, core = place()
+    return (ctx, lax.rem(x, 4) * 2 + y, core)
 
 
 def sibling():
@@ -80,8 +87,8 @@
     return pl.ds(pl.multiple_of(owner * W, 128), W)
 
 
-def head_cols(owner):
-    return pl.ds(pl.multiple_of(owner * HD, 128), HD)
+def group_cols(owner, size):
+    return pl.ds(pl.multiple_of(owner * size * HD, 128), size * HD)
 
 
 def half_rows(core):
@@ -177,16 +184,66 @@
 
 
 class Share:
-    def __init__(self, piece, passed, given, sems, source=None):
+    def __init__(self, piece, passed, given, sems):
         self.piece, self.passed, self.given = piece, passed, given
         self.send, self.recv, self.f_send, self.f_recv = sems
         self.tp = lax.axis_index("tp")
+        self.copies, self.taken = [], []
+        x, y = lax.div(self.tp, 2), lax.rem(self.tp, 2)
+        self.beside = tp_of(x, 1 - y)
+        self.along = [tp_of(x + d, y) for d in range(4)]
+
+        def at(dx, row):
+            return lax.rem(x + dx, 4) * 2 + row
+
+        relay = tuple((3 + d, self.along[d]) for d in (2, 1, 3))
+        self.todo = [(at(0, 1 - y), 0, relay)]
+        for row, base in ((y, 0), (1 - y, 3)):
+            self.todo += [(at(4 - d, row), base + d, ()) for d in (1, 3, 2)]
+
+    def start(self, owner, n, device):
+        here = self.piece(owner)
+        copy = remote(here, here, self.send.at[n], self.recv.at[n], device)
+        copy.start()
+        self.copies.append(copy)
+
+    def push(self):
+        self.start(self.tp, 0, self.beside)
+        for d in (2, 1, 3):
+            self.start(self.tp, d, self.along[d])
+
+    def collect(self, count=NTP):
+        while self.todo and count:
+            owner, n, onward = self.todo.pop(0)
+            here = self.piece(owner)
+            remote(here, here, self.send.at[n], self.recv.at[n], self.beside).wait_recv()
+            for later, device in onward:
+                self.start(owner, later, device)
+            count -= 1
+            if self.passed is None:
+                continue
+            part = self.passed(owner)
+            copy = remote(part, part, self.f_send.at[n], self.f_recv.at[n], sibling())
+            copy.start()
+            self.copies.append(copy)
+            self.taken.append((owner, n))
+
+    def finish(self):
+        self.collect()
+        for owner, n in self.taken:
+            part = self.given(owner)
+            remote(part, part, self.f_send.at[n], self.f_recv.at[n], sibling()).wait_recv()
+
+    def drain(self):
+        for copy in self.copies:
+            copy.wait_send()
+
+
+class Exchange(Share):
+    def __init__(self, piece, passed, given, sems, source=None):
+        super().__init__(piece, passed, given, sems)
         self.source = source or (lambda i: piece(self.tp))
-        self.copies = []
-        self.next = 1
-
-    def owner(self, i):
-        return lax.rem(self.tp - i + NTP, NTP)
+        self.todo = [(lax.rem(self.tp - i + NTP, NTP), i, ()) for i in range(1, NTP)]
 
     def push(self):
         for i in range(1, NTP):
@@ -196,27 +253,6 @@
             copy.start()
             self.copies.append(copy)
 
-    def collect(self, count=NTP):
-        while self.next < NTP and count:
-            i, owner = self.next, self.owner(self.next)
-            here = self.piece(owner)
-            remote(here, here, self.send.at[i], self.recv.at[i], tp_at(i)).wait_recv()
-            part = self.passed(owner)
-            copy = remote(part, part, self.f_send.at[i], self.f_recv.at[i], sibling())
-            copy.start()
-            self.copies.append(copy)
-            self.next, count = self.next + 1, count - 1
-
-    def finish(self):
-        self.collect()
-        for i in range(1, NTP):
-            part = self.given(self.owner(i))
-            remote(part, part, self.f_send.at[i], self.f_recv.at[i], sibling()).wait_recv()
-
-    def drain(self):
-        for copy in self.copies:
-            copy.wait_send()
-
 
 def gelu_pair(pre, tan_pre):
     c = math.sqrt(2.0 / math.pi)
@@ -242,17 +278,18 @@
 def body(
     lat, probes, mod, gains, pattern, wqkv_hbm, wout_hbm, wup_hbm, wdn_hbm,
     lat_out, dens_out,
-    kv_0, kv_1, kv_2, kv_3, kv_4, kv_5,
-    wqkv, wo, wmlp, x, xa_0, xa_1, xa_2, signs, proj, queries, hid, acc, part, got, tot, stat, dens,
+    kv_0, kv_1, kv_2, kv_3,
+    wqkv, wo, wmlp, x, xa_0, xa_1, sg, signs, proj, queries, hid, acc, part, got, cross, tot, stat, dens,
     w_sem, s_send, s_recv, r_send, r_recv, p_send, p_recv, d_send, d_recv,
     *many_sems,
 ):
     ring_sems, share_sems = many_sems[:4], many_sems[4:]
     ctx, tp, core = place()
+    column, y = lax.div(tp, 2), lax.rem(tp, 2)
     mine = feature_cols(tp)
     rows_sent = pl.ds(pl.multiple_of(core * HALF, HALF), 3 * HALF)
-    my_half = pl.ds(pl.multiple_of(core * HALF, HALF), HALF)
-    other_half = pl.ds(pl.multiple_of((1 - core) * HALF, HALF), HALF)
+    my_half = pl.ds(pl.multiple_of(core * (W // 2), HALF), W // 2)
+    other_half = pl.ds(pl.multiple_of((1 - core) * (W // 2), HALF), W // 2)
     full = float(D)
     shard = pl.ds(pl.multiple_of(ctx * SHARD, 64), SHARD)
     loads = [
@@ -261,7 +298,7 @@
         pltpu.make_async_copy(wqkv_hbm.at[1], wqkv.at[:, 0:W], w_sem.at[2]),
         pltpu.make_async_copy(wqkv_hbm.at[2], wqkv.at[:, W : 2 * W], w_sem.at[3]),
         pltpu.make_async_copy(wqkv_hbm.at[0], wqkv.at[:, 2 * W : 3 * W], w_sem.at[4]),
-        pltpu.make_async_copy(wout_hbm.at[:, :, mine], wo.at[:, tp], w_sem.at[5]),
+        pltpu.make_async_copy(wout_hbm.at[:, mine], wo.at[tp], w_sem.at[5]),
     ]
     for load in loads:
         load.start()
@@ -271,21 +308,30 @@
     greet([tp_at(i) for i in range(1, NTP)] + [right, left, across, sibling()])
 
     def block_rows(block, part):
-        return pl.ds(pl.multiple_of(block * SHARD + part * (SHARD // 2), 32), SHARD // 2)
+        start = block * SHARD + part * (SHARD - HALF)
+        return pl.ds(pl.multiple_of(start, HALF), HALF if part else SHARD - HALF)
 
     weight_ring = Ring(
         lambda block, part: wmlp.at[core, block_rows(block, part)],
         lambda block, part: wmlp.at[core, block_rows(block, part)],
         lambda block, part: wmlp.at[1 - core, block_rows(block, part)],
-        [sems.at[STEPS * HEADS] for sems in ring_sems],
+        [sems.at[STEPS * NG] for sems in ring_sems],
     )
-    wout_share = Share(
-        lambda owner: wo.at[:, owner, my_half],
-        lambda owner: wo.at[:, owner, my_half],
-        lambda owner: wo.at[:, owner, other_half],
-        [sems.at[STEPS * (HEADS + 1)] for sems in share_sems],
-        lambda i: wout_hbm.at[:, my_half, feature_cols(lax.rem(tp + i, NTP))],
+    wout_share = Exchange(
+        lambda owner: wo.at[owner, my_half],
+        lambda owner: wo.at[owner, my_half],
+        lambda owner: wo.at[owner, other_half],
+        [sems.at[STEPS * (NG + 1)] for sems in share_sems],
+        lambda i: wout_hbm.at[my_half, feature_cols(lax.rem(tp + i, NTP))],
     )
+    sg[:, mine] = signs[...].astype(BF16)
+    sign_share = Exchange(
+        lambda owner: sg.at[:, feature_cols(owner)],
+        None,
+        None,
+        [sems.at[STEPS * (NG + 1) + 1] for sems in share_sems],
+    )
+    sign_share.push()
     loads[0].wait()
     loads[1].wait()
     weight_ring.start()
@@ -293,8 +339,8 @@
 
     for step in range(STEPS):
         copies = []
-        kvs = (kv_0, kv_1, kv_2, kv_3, kv_4, kv_5)[HEADS * step : HEADS * (step + 1)]
-        xas = (xa_0, xa_1, xa_2)
+        kvs = (kv_0, kv_1, kv_2, kv_3)[NG * step : NG * (step + 1)]
+        xas = (xa_0, xa_1)
         rows, tangent = lat_out[...], signs[...]
         stat[tp] = columns_to_rows(
             [
@@ -322,16 +368,12 @@
         tan_var = 2.0 * (tan_sq - row_mean * tan_mean)
         inv_std = lax.rsqrt(row_var + EPS)
         centred = rows - row_mean
-        shift, gain = mod[3 * step : 3 * step + 1], 1.0 + mod[3 * step + 1 : 3 * step + 2]
+        shift, gain = mod[3 * step : 3 * step + 1, mine], 1.0 + mod[3 * step + 1 : 3 * step + 2, mine]
         normed = (centred * inv_std * gain + shift).astype(BF16)
-        tan_normed = (tangent - tan_mean) * inv_std - 0.5 * centred * (
-            inv_std * inv_std * inv_std * tan_var
-        )
         x[0:HALF, mine] = normed[0:HALF]
-        x[HALF : 3 * HALF, mine] = (tan_normed * gain).astype(BF16)
         x[3 * HALF : ROWS, mine] = normed[HALF:BLK]
-        x_share = Share(
-            lambda owner: x.at[rows_sent, feature_cols(owner)],
+        x_share = Exchange(
+            lambda owner: x.at[half_rows(core), feature_cols(owner)],
             lambda owner: x.at[half_rows(core), feature_cols(owner)],
             lambda owner: x.at[half_rows(1 - core), feature_cols(owner)],
             [sems.at[step] for sems in share_sems],
@@ -339,10 +381,22 @@
         x_share.push()
         if step == 0:
             weight_ring.advance(2)
-            for _ in range(3):
-                x_share.collect(2)
-                weight_ring.advance(2)
+            sign_share.finish()
+            weight_ring.advance(2)
+            x_share.collect(4)
+            weight_ring.advance(2)
         x_share.finish()
+        inv_rows = jnp.broadcast_to(inv_std, (BLK, W))
+        mean_rows = jnp.broadcast_to(inv_std * tan_mean, (BLK, W))
+        var_rows = jnp.broadcast_to(0.5 * inv_std * inv_std * tan_var, (BLK, W))
+        for n in range(NTP):
+            cols = slice(n * W, (n + 1) * W)
+            primal = jnp.concatenate([x[0:HALF, cols], x[3 * HALF : ROWS, cols]], axis=0)
+            scaled = primal.astype(F32) - mod[3 * step : 3 * step + 1, cols]
+            turned = (inv_rows * sg[:, cols].astype(F32) - mean_rows) * (
+                1.0 + mod[3 * step + 1 : 3 * step + 2, cols]
+            )
+            x[HALF : 3 * HALF, cols] = (turned - var_rows * scaled).astype(BF16)
         if step == 0:
             for load in loads[2:]:
                 load.wait()
@@ -364,15 +418,16 @@
                 x[...], wqkv[:, start:stop], preferred_element_type=F32
             )
 
-        def own_block(h):
-            kv = kvs[h]
-            key, tan_key = head_pair(0, 1, h)
-            cols = slice(W + h * HD, W + (h + 1) * HD)
-            kv[ctx, 0] = key
-            kv[ctx, 1] = tan_key
-            kv[ctx, 2] = proj[HALF : 3 * HALF, cols].astype(BF16)
-            kv[ctx, 3, 0:HALF] = proj[0:HALF, cols].astype(BF16)
-            kv[ctx, 3, HALF:BLK] = proj[3 * HALF : ROWS, cols].astype(BF16)
+        def own_block(g):
+            kv = kvs[g]
+            for n, h in enumerate(GROUPS[g]):
+                key, tan_key = head_pair(0, 1, h)
+                cols, to = slice(W + h * HD, W + (h + 1) * HD), slice(n * HD, (n + 1) * HD)
+                kv[ctx, 0, :, to] = key
+                kv[ctx, 1, :, to] = tan_key
+                kv[ctx, 2, :, to] = proj[HALF : 3 * HALF, cols].astype(BF16)
+                kv[ctx, 3, 0:HALF, to] = proj[0:HALF, cols].astype(BF16)
+                kv[ctx, 3, HALF:BLK, to] = proj[3 * HALF : ROWS, cols].astype(BF16)
 
         def part_rows(part):
             return slice(part * HALF, (part + 1) * HALF)
@@ -382,18 +437,20 @@
                 lambda block, part, kv=kv: kv.at[block, pl.ds(core, 3), part_rows(part)],
                 lambda block, part, kv=kv: kv.at[block, pl.ds(core * 3, 1), part_rows(part)],
                 lambda block, part, kv=kv: kv.at[block, pl.ds((1 - core) * 3, 1), part_rows(part)],
-                [sems.at[step * HEADS + h] for sems in ring_sems],
+                [sems.at[step * NG + g] for sems in ring_sems],
             )
-            for h, kv in enumerate(kvs)
+            for g, kv in enumerate(kvs)
         ]
         shares = [
-            Share(
-                lambda owner, xa=xa: xa.at[rows_sent, head_cols(owner)],
-                lambda owner, xa=xa: xa.at[half_rows(core), head_cols(owner)],
-                lambda owner, xa=xa: xa.at[half_rows(1 - core), head_cols(owner)],
-                [sems.at[STEPS + step * HEADS + h] for sems in share_sems],
+            (Share, Exchange)[g](
+                lambda owner, xa=xa, g=g: xa.at[rows_sent, group_cols(owner, len(GROUPS[g]))],
+                lambda owner, xa=xa, g=g: xa.at[half_rows(core), group_cols(owner, len(GROUPS[g]))],
+                lambda owner, xa=xa, g=g: xa.at[
+                    half_rows(1 - core), group_cols(owner, len(GROUPS[g]))
+                ],
+                [sems.at[STEPS + step * NG + g] for sems in share_sems],
             )
-            for h, xa in enumerate(xas)
+            for g, xa in enumerate(xas)
         ]
         for n in range(3):
             project(256 * n, 256 * (n + 1))
@@ -403,7 +460,6 @@
             weight_ring.advance(4)
             wout_share.push()
         own_block(1)
-        own_block(2)
         project(768, 1152)
         for h in range(HEADS):
             query, tan_query = head_pair(768, 0, h)
@@ -415,17 +471,6 @@
                 rings[0].advance(1)
             weight_ring.finish()
 
-        spread = 15
-        agenda = []
-        for h in range(HEADS):
-            size = 2 + 28
-            for k in range(size - len(rings[h].todo), size):
-                agenda.append((k + spread * h, 1, h, "advance"))
-            if h:
-                agenda.append((spread * h - 6, 0, h, "start"))
-            agenda.append((size + spread * h, 2, h, "attend"))
-        agenda.sort()
-
         def up(n):
             cols = slice(256 * n, 256 * (n + 1))
             pre = jnp.dot(x[...], wmlp[0, :, cols], preferred_element_type=F32)
@@ -436,30 +481,50 @@
             hid[HALF : 3 * HALF, cols] = tan_hidden.astype(BF16)
             hid[3 * HALF : ROWS, cols] = hidden[HALF:BLK]
 
-        def down(i):
-            units = feature_cols(lax.rem(tp + i, NTP))
-            part[i % NTP] = lax.dot_general(
+        def down(d, k):
+            row = y if k == 0 else 1 - y
+            units = feature_cols(lax.rem(column + d, 4) * 2 + row)
+            part[d, k] = lax.dot_general(
                 hid[...], wmlp[1, units, :], (((1,), (1,)), ((), ())), preferred_element_type=F32
             ).astype(BF16)
-            if i < NTP:
+            if d and k:
                 copy = remote(
-                    part.at[i, rows_sent],
-                    got.at[i],
-                    r_send.at[step, i],
-                    r_recv.at[step, i],
-                    tp_at(i),
+                    part.at[d, :, rows_sent],
+                    got.at[d - 1],
+                    r_send.at[step, d],
+                    r_recv.at[step, d],
+                    tp_of(column + d, y),
                 )
                 copy.start()
                 copies.append(copy)
 
+        def collect_column():
+            for d in range(1, 4):
+                remote(
+                    got.at[d - 1], got.at[d - 1], r_send.at[step, d], r_recv.at[step, d], sibling()
+                ).wait_recv()
+            total = part[0, 1, rows_sent].astype(F32)
+            for d in range(3):
+                total = total + got[d, 1].astype(F32)
+            cross[0] = total.astype(BF16)
+            copy = remote(
+                cross.at[0],
+                cross.at[1],
+                r_send.at[step, 0],
+                r_recv.at[step, 0],
+                tp_of(column, 1 - y),
+            )
+            copy.start()
+            copies.append(copy)
+
         def collect_parts():
-            total = part[0, rows_sent].astype(F32)
-            for i in range(1, NTP):
-                remote(
-                    got.at[i], got.at[i], r_send.at[step, i], r_recv.at[step, i], tp_at(i)
-                ).wait_recv()
-                total = total + got[i].astype(F32)
-            tot[rows_sent] = total
+            total = part[0, 0, rows_sent].astype(F32)
+            for d in range(3):
+                total = total + got[d, 0].astype(F32)
+            remote(
+                cross.at[1], cross.at[1], r_send.at[step, 0], r_recv.at[step, 0], sibling()
+            ).wait_recv()
+            tot[rows_sent] = total + cross[1].astype(F32)
             piece = tot.at[half_rows(core)]
             copy = remote(piece, piece, p_send.at[step], p_recv.at[step], sibling())
             copy.start()
@@ -474,19 +539,20 @@
         scale = 1.0 / math.sqrt(HD)
         contract = (((1,), (1,)), ((), ()))
 
-        def attend(h):
-            kv, xa = kvs[h], xas[h]
+        def attend(g, n):
+            kv, xa, h = kvs[g], xas[g], GROUPS[g][n]
+            own = slice(n * HD, (n + 1) * HD)
             pair = queries[:, h * HD : (h + 1) * HD]
             scores, tan_scores = [], []
             for j in range(K_SEL):
-                key, tan_key = kv[listed[j], 0], kv[listed[j], 1]
+                key, tan_key = kv[listed[j], 0, :, own], kv[listed[j], 1, :, own]
                 both = lax.dot_general(pair, key, contract, preferred_element_type=F32) * scale
-                cross = lax.dot_general(
+                crossed = lax.dot_general(
                     pair[0:BLK], tan_key, contract, preferred_element_type=F32
                 )
                 score = both[0:BLK]
                 scores.append(score + penalty[j] if j else score)
-                tan_scores.append(both[BLK:ROWS] + cross * scale)
+                tan_scores.append(both[BLK:ROWS] + crossed * scale)
             top = scores[0]
             for j in range(1, K_SEL):
                 top = jnp.maximum(top, scores[j])
@@ -498,54 +564,58 @@
                 weighted = weights * tan_scores[j]
                 weight_sum, tan_sum = weight_sum + weights, tan_sum + weighted
                 left_side = jnp.concatenate([weights, weighted], axis=0).astype(BF16)
-                values = jnp.concatenate([kv[listed[j], 3], kv[listed[j], 2]], axis=1)
+                values = jnp.concatenate(
+                    [kv[listed[j], 3, :, own], kv[listed[j], 2, :, own]], axis=1
+                )
                 out = out + jnp.dot(left_side, values, preferred_element_type=F32)
             inv = 1.0 / jnp.sum(weight_sum, 1, keepdims=True)
             ratio = jnp.sum(tan_sum, 1, keepdims=True) * inv
             output = out[0:BLK, 0:HD] * inv
             tan_output = (out[0:BLK, HD : 2 * HD] + out[BLK:ROWS, 0:HD]) * inv - ratio * output
             output = output.astype(BF16)
-            cols = head_cols(tp)
+            cols = pl.ds(pl.multiple_of((tp * len(GROUPS[g]) + n) * HD, 128), HD)
             xa[0:HALF, cols] = output[0:HALF]
             xa[HALF : 3 * HALF, cols] = tan_output.astype(BF16)
             xa[3 * HALF : ROWS, cols] = output[HALF:BLK]
-            shares[h].push()
-
-        def out_project(h):
-            more = jnp.dot(
-                xas[h][...], wo[h].reshape(NTP * HD, W), preferred_element_type=F32
-            )
-            acc[...] = more if h == 0 else acc[...] + more
-
-        tasks = [partial(up, n) for n in range(3)] + [partial(down, i) for i in range(1, NTP + 1)]
-        done = 0
-        for _, _, h, what in agenda:
-            if what == "start":
-                rings[h].start()
-            elif what == "advance":
-                rings[h].advance(1)
-                done += 1
-                if tasks and done % 2 == 0:
-                    tasks.pop(0)()
-            else:
-                rings[h].finish()
-                while h == 0 and tasks:
-                    tasks.pop(0)()
-                attend(h)
-                if h == 0 and step == 0:
-                    wout_share.finish()
-                if h == 1:
-                    shares[0].finish()
-                    out_project(0)
-                    collect_parts()
+
+        def out_project(g):
+            size = len(GROUPS[g]) * HD
+            rows = wo[:, GROUPS[g][0] * HD : GROUPS[g][0] * HD + size].reshape(NTP * size, W)
+            more = jnp.dot(xas[g][...], rows, preferred_element_type=F32)
+            acc[...] = more if g == 0 else acc[...] + more
+
+        tasks = [partial(up, n) for n in range(3)] + [
+            partial(down, d, k) for d in (2, 1, 3, 0) for k in (0, 1)
+        ]
+        had = 30 - len(rings[0].todo)
+        agenda = [(k, 1, rings[0].advance) for k in range(had, 30)]
+        agenda += [(max(9, had), 0, rings[1].start)]
+        agenda += [(15 + k, 2, rings[1].advance) for k in range(30)]
+        agenda += [(had + 1 + n * (1.6 if step else 1.1), 3, task) for n, task in enumerate(tasks)]
+        agenda += [
+            (30, 4, rings[0].finish),
+            (30, 5, partial(attend, 0, 0)),
+            (33, 5, partial(attend, 0, 1)),
+            (33, 6, shares[0].push),
+            (36, 5, collect_column),
+            (38, 5, partial(shares[0].collect, 1)),
+            (45, 5, rings[1].finish),
+            (45, 6, partial(attend, 1, 0)),
+            (45, 7, shares[1].push),
+            (46, 0, shares[0].finish),
+            (46, 1, collect_parts),
+        ]
+        if step == 0:
+            agenda.append((35, 5, wout_share.finish))
+        for _, _, task in sorted(agenda, key=lambda entry: entry[:2]):
+            task()
+        out_project(0)
+        other = tot.at[half_rows(1 - core)]
+        remote(other, other, p_send.at[step], p_recv.at[step], sibling()).wait_recv()
         shares[1].finish()
         out_project(1)
-        other = tot.at[half_rows(1 - core)]
-        remote(other, other, p_send.at[step], p_recv.at[step], sibling()).wait_recv()
-        shares[2].finish()
-        out_project(2)
         branch = acc[...] + tot[...]
-        gate = mod[3 * step + 2 : 3 * step + 3]
+        gate = mod[3 * step + 2 : 3 * step + 3, mine]
         change = change + jnp.sum(
             signs[...] * (gate * branch[HALF : 3 * HALF]), axis=1, keepdims=True
         )
@@ -553,7 +623,7 @@
         lat_out[HALF:BLK] += (1.0 / STEPS) * (gate * branch[3 * HALF : ROWS])
         for copy in copies:
             copy.wait_send()
-        for part_of in rings + shares + [x_share] + ([weight_ring, wout_share] if step == 0 else []):
+        for part_of in rings + shares + [x_share] + ([weight_ring, wout_share, sign_share] if step == 0 else []):
             part_of.drain()
 
     copies = []
@@ -579,8 +649,7 @@
 
 
 def local(latent, probes, modulation, pattern, w_qkv, w_out, w_up, w_down, q_gain, k_gain):
-    start = lax.axis_index("tp") * W
-    mod = lax.dynamic_slice_in_dim(modulation.reshape(3 * STEPS, D), start, W, 1)
+    mod = modulation.reshape(3 * STEPS, D)
     gains = jnp.stack([q_gain, k_gain])
     vmem, anywhere = pl.BlockSpec(memory_space=pltpu.VMEM), pl.BlockSpec(memory_space=pl.ANY)
     dma = pltpu.SemaphoreType.DMA
@@ -592,22 +661,27 @@
         ),
         in_specs=[vmem] * 4 + [pl.BlockSpec(memory_space=pltpu.SMEM)] + [anywhere] * 4,
         out_specs=(vmem, vmem),
-        scratch_shapes=[pltpu.VMEM((NCTX, 4, BLK, HD), BF16) for _ in range(STEPS * HEADS)]
+        scratch_shapes=[
+            pltpu.VMEM((NCTX, 4, BLK, len(group) * HD), BF16)
+            for _ in range(STEPS)
+            for group in GROUPS
+        ]
         + [
             pltpu.VMEM((D, 3 * W), BF16),
-            pltpu.VMEM((HEADS, NTP, HD, W), BF16),
+            pltpu.VMEM((NTP, W, W), BF16),
             pltpu.VMEM((2, D, UNITS), BF16),
             pltpu.VMEM((ROWS, D), BF16),
-            pltpu.VMEM((ROWS, NTP * HD), BF16),
-            pltpu.VMEM((ROWS, NTP * HD), BF16),
-            pltpu.VMEM((ROWS, NTP * HD), BF16),
+            pltpu.VMEM((ROWS, NTP * len(GROUPS[0]) * HD), BF16),
+            pltpu.VMEM((ROWS, NTP * len(GROUPS[1]) * HD), BF16),
+            pltpu.VMEM((BLK, D), BF16),
             pltpu.VMEM((BLK, W), F32),
             pltpu.VMEM((ROWS, 3 * W), F32),
             pltpu.VMEM((ROWS, W), BF16),
             pltpu.VMEM((ROWS, UNITS), BF16),
             pltpu.VMEM((ROWS, W), F32),
-            pltpu.VMEM((NTP, ROWS, W), BF16),
-            pltpu.VMEM((NTP, 3 * HALF, W), BF16),
+            pltpu.VMEM((4, 2, ROWS, W), BF16),
+            pltpu.VMEM((3, 2, 3 * HALF, W), BF16),
+            pltpu.VMEM((2, 3 * HALF, W), BF16),
             pltpu.VMEM((ROWS, W), F32),
             pltpu.VMEM((NTP, 8, BLK), F32),
             pltpu.VMEM((NTP + 2, 8, BLK), F32),
@@ -616,8 +690,8 @@
         + [dma((STEPS, NTP)) for _ in range(4)]
         + [dma((STEPS,)) for _ in range(2)]
         + [dma((NTP,)) for _ in range(2)]
-        + [dma((STEPS * HEADS + 1, 30)) for _ in range(4)]
-        + [dma((STEPS * (HEADS + 1) + 1, NTP)) for _ in range(4)],
+        + [dma((STEPS * NG + 1, 30)) for _ in range(4)]
+        + [dma((STEPS * (NG + 1) + 2, NTP)) for _ in range(4)],
         compiler_params=pltpu.CompilerParams(
             collective_id=1, has_side_effects=True, vmem_limit_bytes=60 * 1024 * 1024
         ),
@@ -629,7 +703,7 @@
         gains,
         pattern,
         w_qkv.transpose(1, 0, 2),
-        w_out.reshape(HEADS, HD, D),
+        w_out,
         w_up,
         w_down.T,
     )

time: 277 us -> 226 us (0.82)
  Pallas kernels: 270 us -> 219 us
    pallas_call x1, Pallas kernels: 270 us -> 219 us  [local(): pl.pallas_call(body, out_shape=(jax.ShapeDtypeStruct((BLK, W), F32), jax....]
where the time goes in v4:
time: 226 us
  Pallas kernels  219 us (97%)
  local copies, waits for them, and re-layouts  5.76 us (3%)
    pallas_call x1, Pallas kernels, local(): pl.pallas_call(body, out_shape=(jax.ShapeDtypeStruct((BLK, W), F32), jax....  219 us

profile of v4, /device:TPU:1, one launch (start us, length us, event | category | flops | bytes accessed | tf_op | source)
XLA Modules:
  0.0 226.2 jit_solution(2882037420709644008)
XLA Ops:
  0.6 0.7 stack.9
  1.3 0.7 stack.10
  2.0 0.6 pad_maximum_fusion.gains
  2.6 0.9 copy.13
  3.5 0.7 reshape.7.mod
  4.2 219.2 %euler_steps.1 = (f32[128,384]{1,0:T(8,128)}, f32[8,128]{1,0:T(8,128)}) custom-call(f32[128,384]{1,0:T(8,128)} %lat.1, s32[128,384]{1,0:T(8,128)} %bitcast.7, f32[6,3072]{1,0:T(8,128)} %reshape.7.mod, f32[2,384]{1,0:T(2,128)} %pad_maximum_fusion.gains, s32[1,8]{1,0:T(1,128)} %pattern.1, bf16[3,3072,384]{2,1,0:T(8,128)(2,1)} %bitcast.5, ...), custom_call_target="tpu_custom_call" | custom-call | tf_op jit(solution)/shard_map/euler_steps/pallas_call | solution.py:656
  223.4 1.2 slice_bitcast_fusion
  224.6 1.6 copy.15

commit v5 on v4

--- a/solution.py
+++ b/solution.py
@@ -228,6 +228,12 @@
             self.copies.append(copy)
             self.taken.append((owner, n))
 
+    def settle(self):
+        owner, n = self.taken.pop(0)
+        part = self.given(owner)
+        remote(part, part, self.f_send.at[n], self.f_recv.at[n], sibling()).wait_recv()
+        return owner
+
     def finish(self):
         self.collect()
         for owner, n in self.taken:
@@ -295,8 +301,10 @@
     loads = [
         pltpu.make_async_copy(wup_hbm, wmlp.at[0, shard], w_sem.at[0]),
         pltpu.make_async_copy(wdn_hbm, wmlp.at[1, shard], w_sem.at[1]),
-        pltpu.make_async_copy(wqkv_hbm.at[1], wqkv.at[:, 0:W], w_sem.at[2]),
-        pltpu.make_async_copy(wqkv_hbm.at[2], wqkv.at[:, W : 2 * W], w_sem.at[3]),
+        pltpu.make_async_copy(wqkv_hbm.at[1, :, 0:256], wqkv.at[:, 0:256], w_sem.at[2]),
+        pltpu.make_async_copy(wqkv_hbm.at[2, :, 0:256], wqkv.at[:, 256:512], w_sem.at[3]),
+        pltpu.make_async_copy(wqkv_hbm.at[1, :, 256:W], wqkv.at[:, 512:640], w_sem.at[6]),
+        pltpu.make_async_copy(wqkv_hbm.at[2, :, 256:W], wqkv.at[:, 640:768], w_sem.at[7]),
         pltpu.make_async_copy(wqkv_hbm.at[0], wqkv.at[:, 2 * W : 3 * W], w_sem.at[4]),
         pltpu.make_async_copy(wout_hbm.at[:, mine], wo.at[tp], w_sem.at[5]),
     ]
@@ -383,26 +391,32 @@
             weight_ring.advance(2)
             sign_share.finish()
             weight_ring.advance(2)
-            x_share.collect(4)
-            weight_ring.advance(2)
-        x_share.finish()
         inv_rows = jnp.broadcast_to(inv_std, (BLK, W))
         mean_rows = jnp.broadcast_to(inv_std * tan_mean, (BLK, W))
         var_rows = jnp.broadcast_to(0.5 * inv_std * inv_std * tan_var, (BLK, W))
-        for n in range(NTP):
-            cols = slice(n * W, (n + 1) * W)
+
+        def rebuild(cols):
             primal = jnp.concatenate([x[0:HALF, cols], x[3 * HALF : ROWS, cols]], axis=0)
             scaled = primal.astype(F32) - mod[3 * step : 3 * step + 1, cols]
             turned = (inv_rows * sg[:, cols].astype(F32) - mean_rows) * (
                 1.0 + mod[3 * step + 1 : 3 * step + 2, cols]
             )
             x[HALF : 3 * HALF, cols] = (turned - var_rows * scaled).astype(BF16)
+
+        rebuild(mine)
+        for i in range(1, NTP):
+            x_share.collect(1)
+            if step == 0 and i == 4:
+                weight_ring.advance(2)
+            if i > 1:
+                rebuild(feature_cols(x_share.settle()))
+        rebuild(feature_cols(x_share.settle()))
         if step == 0:
             for load in loads[2:]:
                 load.wait()
 
         def head_pair(column, gain_row, h):
-            view = proj[:, column + h * HD : column + (h + 1) * HD]
+            view = proj[:, column : column + HD]
             primal = jnp.concatenate([view[0:HALF], view[3 * HALF : ROWS]], axis=0)
             tan = view[HALF : 3 * HALF]
             gain_view = gains[gain_row : gain_row + 1, h * HD : (h + 1) * HD]
@@ -421,8 +435,9 @@
         def own_block(g):
             kv = kvs[g]
             for n, h in enumerate(GROUPS[g]):
-                key, tan_key = head_pair(0, 1, h)
-                cols, to = slice(W + h * HD, W + (h + 1) * HD), slice(n * HD, (n + 1) * HD)
+                key_at, value_at = (h * HD, 256 + h * HD) if g == 0 else (512, 640)
+                key, tan_key = head_pair(key_at, 1, h)
+                cols, to = slice(value_at, value_at + HD), slice(n * HD, (n + 1) * HD)
                 kv[ctx, 0, :, to] = key
                 kv[ctx, 1, :, to] = tan_key
                 kv[ctx, 2, :, to] = proj[HALF : 3 * HALF, cols].astype(BF16)
@@ -452,17 +467,18 @@
             )
             for g, xa in enumerate(xas)
         ]
-        for n in range(3):
-            project(256 * n, 256 * (n + 1))
+        project(0, 256)
+        project(256, 512)
         own_block(0)
         rings[0].start()
         if step == 0:
             weight_ring.advance(4)
             wout_share.push()
+        project(512, 768)
         own_block(1)
         project(768, 1152)
         for h in range(HEADS):
-            query, tan_query = head_pair(768, 0, h)
+            query, tan_query = head_pair(768 + h * HD, 0, h)
             queries[0:BLK, h * HD : (h + 1) * HD] = query
             queries[BLK:ROWS, h * HD : (h + 1) * HD] = tan_query
         if step == 0:
@@ -606,7 +622,7 @@
             (46, 1, collect_parts),
         ]
         if step == 0:
-            agenda.append((35, 5, wout_share.finish))
+            agenda += [(40, 5, wout_share.collect), (46, 2, wout_share.finish)]
         for _, _, task in sorted(agenda, key=lambda entry: entry[:2]):
             task()
         out_project(0)
@@ -685,7 +701,7 @@
             pltpu.VMEM((ROWS, W), F32),
             pltpu.VMEM((NTP, 8, BLK), F32),
             pltpu.VMEM((NTP + 2, 8, BLK), F32),
-            dma((6,)),
+            dma((8,)),
         ]
         + [dma((STEPS, NTP)) for _ in range(4)]
         + [dma((STEPS,)) for _ in range(2)]

time: 226 us -> 226 us (level)
  no operation moved by 1% of the time
where the time goes in v5:
time: 226 us
  Pallas kernels  219 us (97%)
  local copies, waits for them, and re-layouts  5.76 us (3%)
    pallas_call x1, Pallas kernels, local(): pl.pallas_call(body, out_shape=(jax.ShapeDtypeStruct((BLK, W), F32), jax....  219 us

profile of v5, /device:TPU:1, one launch (start us, length us, event | category | flops | bytes accessed | tf_op | source)
XLA Modules:
  0.0 225.7 jit_solution(18443167082662847361)
XLA Ops:
  0.6 0.7 stack.9
  1.3 0.7 stack.10
  2.0 0.6 pad_maximum_fusion.gains
  2.6 0.9 copy.13
  3.5 0.7 reshape.7.mod
  4.2 218.7 %euler_steps.1 = (f32[128,384]{1,0:T(8,128)}, f32[8,128]{1,0:T(8,128)}) custom-call(f32[128,384]{1,0:T(8,128)} %lat.1, s32[128,384]{1,0:T(8,128)} %bitcast.7, f32[6,3072]{1,0:T(8,128)} %reshape.7.mod, f32[2,384]{1,0:T(2,128)} %pad_maximum_fusion.gains, s32[1,8]{1,0:T(1,128)} %pattern.1, bf16[3,3072,384]{2,1,0:T(8,128)(2,1)} %bitcast.5, ...), custom_call_target="tpu_custom_call" | custom-call | tf_op jit(solution)/shard_map/euler_steps/pallas_call | solution.py:672
  222.9 1.2 slice_bitcast_fusion
  224.0 1.6 copy.15
